TPU v7x, 256 devices: a whole 4x4x8 slice. The times are simulated.
256 devices in a mesh: row: 8 (over x, y_lo), col: 32 (over y_hi, z, core).
Axes of the slice: x: 4, y: 4 (y_hi: 2, y_lo: 2; y = y_hi * 2 + y_lo), z: 8, core: 2. Of those that a mesh axis runs over, the one named last changes fastest.
Arguments:
- mlp_param: float32 [6144, 24576], P('row', 'col'), may hold values from -250 to 250
- mlp_grad: bfloat16 [6144, 24576], P('row', 'col'), may hold values from -250 to 250
- mlp_row_state: float32 [6144], P('row'), may hold values from 0.03 to 2.7
- mlp_col_state: float32 [24576], P('col'), may hold values from 0.02 to 0.3
- attn_param: float32 [6144, 6144], P('row', 'col'), may hold values from -250 to 250
- attn_grad: bfloat16 [6144, 6144], P('row', 'col'), may hold values from -250 to 250
- attn_row_state: float32 [6144], P('row'), may hold values from 0.03 to 2.7
- attn_col_state: float32 [6144], P('col'), may hold values from 0.02 to 0.3
Outputs:
- mlp_param_new: float32 [6144, 24576], P('row', 'col')
- attn_param_new: float32 [6144, 6144], P('row', 'col')
- mlp_row_new: float32 [6144], P('row')
- mlp_col_new: float32 [24576], P('col')
- attn_row_new: float32 [6144], P('row')
- attn_col_new: float32 [6144], P('col')
- attn_copy: bfloat16 [6144, 6144], P(None, 'col')
All inputs are finite; a program needn't handle non-finite values.
Results may differ from a plain program's by a relative error of at most 0.0004.
Values may be sent and summed in bfloat16 or wider, within the bound.
No kernel may reach another device: no remote copies, remote signals or barrier semaphores. Data moves between devices by JAX's collectives and lax.ppermute only.
A program may use at most 64 MiB of HBM per device.

v0:
```python
import jax
import jax.numpy as jnp
from jax import lax
from jax.sharding import Mesh
from jax.sharding import PartitionSpec as P

STEP = 4
ROW = ("row_0", "row_1")
COL = ("col_0", "col_1", "col_2")
ROW_COL = ("row_0", "row_1", "col_0", "col_1", "col_2")


TINY_SQUARE = 1e-30
LEARN_RATE = 0.05
DECAY_POWER = 0.8


def over_axes(value, axes):
    for axis in axes:
        value = lax.psum(value, axis)
    return value


def from_everyone(value, axis):
    length = lax.axis_size(axis)
    return lax.all_to_all(
        jnp.broadcast_to(value[None], (length, *value.shape)), axis, 0, 0, tiled=True
    )


def of_everyone(value, axis):
    return from_everyone(value, axis).sum(axis=0)


def packed_total(arrays, axis):
    ends = [0]
    for a in arrays:
        ends.append(ends[-1] + a.size)
    running = of_everyone(jnp.concatenate([a.ravel() for a in arrays]), axis)
    return tuple((running[b:e].reshape(a.shape) for a, b, e in zip(arrays, ends, ends[1:])))


def in_order(pieces, dim):
    pieces = jnp.moveaxis(pieces, 0, dim)
    dims = pieces.shape
    return pieces.reshape(*dims[:dim], dims[dim] * dims[dim + 1], *dims[dim + 2 :])


def gather_directly(value, axis, dim):
    pieces = from_everyone(value, axis)
    return in_order(pieces, dim)


def local(
    mlp_param,
    mlp_grad,
    mlp_row_state,
    mlp_col_state,
    attn_param,
    attn_grad,
    attn_row_state,
    attn_col_state,
):
    keep_rate = 1.0 - STEP ** (-DECAY_POWER)
    block_rows = mlp_grad.shape[0]
    rows_total = block_rows * lax.axis_size(ROW)
    mlp_width = mlp_grad.shape[1] * lax.axis_size(COL)
    attn_width = attn_grad.shape[1] * lax.axis_size(COL)
    mlp_count = float(rows_total * mlp_width)
    attn_count = float(rows_total * attn_width)
    mlp_square = jnp.square(mlp_grad.astype(jnp.float32)) + TINY_SQUARE
    attn_square = jnp.square(attn_grad.astype(jnp.float32)) + TINY_SQUARE
    param_local = (jnp.sum(jnp.square(mlp_param)), jnp.sum(jnp.square(attn_param)))
    param_mlp, param_attn = (over_axes(param_local[0], ROW_COL), over_axes(param_local[1], ROW_COL))
    row_mlp, row_attn = packed_total(
        (jnp.sum(mlp_square, axis=1), jnp.sum(attn_square, axis=1)), COL
    )
    mlp_rows_new = keep_rate * mlp_row_state + (1.0 - keep_rate) * (row_mlp / mlp_width)
    attn_rows_new = keep_rate * attn_row_state + (1.0 - keep_rate) * (row_attn / attn_width)
    col_mlp, col_attn = packed_total(
        (jnp.sum(mlp_square, axis=0), jnp.sum(attn_square, axis=0)), ROW
    )
    mlp_cols_new = keep_rate * mlp_col_state + (1.0 - keep_rate) * (col_mlp / rows_total)
    attn_cols_new = keep_rate * attn_col_state + (1.0 - keep_rate) * (col_attn / rows_total)
    mlp_raw = mlp_grad.astype(jnp.float32) / jnp.sqrt(mlp_rows_new[:, None] * mlp_cols_new[None, :])
    attn_raw = attn_grad.astype(jnp.float32) / jnp.sqrt(
        attn_rows_new[:, None] * attn_cols_new[None, :]
    )
    clip_local = (jnp.sum(jnp.square(mlp_raw)), jnp.sum(jnp.square(attn_raw)))
    clip_mlp, clip_attn = (over_axes(clip_local[0], ROW_COL), over_axes(clip_local[1], ROW_COL))
    mlp_clip = jnp.maximum(1.0, jnp.sqrt(clip_mlp / mlp_count))
    attn_clip = jnp.maximum(1.0, jnp.sqrt(clip_attn / attn_count))
    mlp_step = LEARN_RATE * jnp.sqrt(param_mlp / mlp_count)
    attn_step = LEARN_RATE * jnp.sqrt(param_attn / attn_count)
    mlp_new = mlp_param - mlp_step * (mlp_raw / mlp_clip)
    attn_new = attn_param - attn_step * (attn_raw / attn_clip)
    weight_copy = gather_directly(attn_new.astype(jnp.bfloat16), ROW, 0)
    return (
        mlp_new,
        attn_new,
        mlp_rows_new,
        mlp_cols_new,
        attn_rows_new,
        attn_cols_new,
        weight_copy,
    )


def solution(mesh):
    finer = Mesh(mesh.devices.reshape(4, 2, 2, 8, 2), ("row_0", "row_1", "col_0", "col_1", "col_2"))
    return jax.shard_map(
        local,
        mesh=finer,
        in_specs=(
            P(ROW, COL),
            P(ROW, COL),
            P(ROW),
            P(COL),
            P(ROW, COL),
            P(ROW, COL),
            P(ROW),
            P(COL),
        ),
        out_specs=(P(ROW, COL), P(ROW, COL), P(ROW), P(COL), P(ROW), P(COL), P(None, COL)),
        check_vma=False,
    )
```

profile of v0, /device:TPU:1, one launch (start us, length us, event | category | flops | bytes accessed | tf_op | source)
XLA Modules:
  0.0 134.2 jit_solution(17880412056513600817)
XLA Ops:
  0.6 0.0 copy-start
  0.7 0.0 copy-start.8
  0.7 0.0 copy-start.9
  0.7 0.0 copy-start.3
  0.7 1.3 fusion.5
  2.0 1.8 %fusion.2 = (f32[768]{0:T(1024)S(1)}, f32[768]{0:T(1024)S(1)}) fusion(bf16[768,768]{1,0:T(8,128)(2,1)} %param.9), kind=kLoop, calls=%fused_computation.4 | loop fusion | flops 2947584 | bytes 1185792 | tf_op jit(solution)/shard_map/reduce_sum | solution.py:76
  3.8 0.6 broadcast_in_dim.7
  4.5 5.9 %all-to-all-start.1 = ((f32[8,1,960]{2,1,0:T(1,128)}), f32[8,1,960]{2,1,0:T(1,128)S(1)}, u32[]{:S(2)}, u32[]{:S(2)}) async-start(f32[8,1,960]{2,1,0:T(1,128)} %broadcast_in_dim.7), calls=%async_computation.1 | async-start | bytes 65536 | tf_op jit(solution)/shard_map/all_to_all | solution.py:26
  10.3 5.1 %all-to-all-done.1 = f32[8,1,960]{2,1,0:T(1,128)S(1)} async-done(((f32[8,1,960]{2,1,0:T(1,128)}), f32[8,1,960]{2,1,0:T(1,128)S(1)}, u32[]{:S(2)}, u32[]{:S(2)}) %all-to-all-start.1) | async-done | bytes 30752 | tf_op jit(solution)/shard_map/all_to_all | solution.py:26
  15.4 0.8 broadcast_in_dim.6
  16.2 13.0 %all-to-all-start = ((f32[32,1,1536]{2,1,0:T(1,128)}), f32[32,1,1536]{2,1,0:T(1,128)S(1)}, u32[]{:S(2)}, u32[]{:S(2)}) async-start(f32[32,1,1536]{2,1,0:T(1,128)} %broadcast_in_dim.6), calls=%async_computation | async-start | bytes 393216 | tf_op jit(solution)/shard_map/all_to_all | solution.py:26
  29.3 0.7 multiply_add_fusion.1
  29.9 0.7 multiply_add_fusion
  30.6 10.2 %all-to-all-done = f32[32,1,1536]{2,1,0:T(1,128)S(1)} async-done(((f32[32,1,1536]{2,1,0:T(1,128)}), f32[32,1,1536]{2,1,0:T(1,128)S(1)}, u32[]{:S(2)}, u32[]{:S(2)}) %all-to-all-start) | async-done | bytes 196640 | tf_op jit(solution)/shard_map/all_to_all | solution.py:26
  40.8 0.1 reduce_sum.93
  41.0 0.0 copy-done.8
  41.0 0.0 copy-done.9
  41.0 0.0 copy-start.4
  41.0 0.0 copy-start.6
  41.0 0.9 multiply_reduce_fusion.2
  41.9 3.3 %multiply_reduce_fusion = (f32[]{:T(128)}, f32[]{:T(128)}) fusion(bf16[768,768]{1,0:T(8,128)(2,1)S(1)} %copy-done, f32[768]{0:T(1024)S(1)} %multiply_add_fusion, f32[768]{0:T(1024)S(1)} %get-tuple-element.34, f32[768,768]{1,0:T(8,128)} %param.8), kind=kLoop, calls=%fused_computation.6 | loop fusion | flops 4128766 | bytes 3545096 | tf_op jit(solution)/shard_map/reduce_sum | solution.py:89
  45.2 7.6 %all-reduce.1 = (f32[]{:T(128)}, f32[]{:T(128)}, f32[]{:T(128)}, f32[]{:T(128)}) all-reduce(f32[]{:T(128)} %get-tuple-element.35, f32[]{:T(128)} %get-tuple-element.36, f32[]{:T(128)} %get-tuple-element.37, f32[]{:T(128)} %get-tuple-element.38), channel_id=1, replica_groups=mesh['row_0'=4,'row_1'=2,'col_0'=2,'col_1'=8,'col_2'=2] {'row_0'}, use_global_device_ids=true, to_apply=%region_13.0 | all-reduce | flops 4 | bytes 32 | tf_op jit(solution)/shard_map/psum | solution.py:20
  52.8 4.4 %all-reduce.4 = (f32[]{:T(128)}, f32[]{:T(128)}, f32[]{:T(128)}, f32[]{:T(128)}) all-reduce(f32[]{:T(128)} %get-tuple-element.15, f32[]{:T(128)} %get-tuple-element.16, f32[]{:T(128)} %get-tuple-element.17, f32[]{:T(128)} %get-tuple-element.18), channel_id=1, replica_groups=mesh['row_0'=4,'row_1'=2,'col_0'=2,'col_1'=8,'col_2'=2] {'row_1'}, use_global_device_ids=true, to_apply=%region_14.0 | all-reduce | flops 4 | bytes 32 | tf_op jit(solution)/shard_map/psum | solution.py:20
  57.2 5.9 %all-reduce.3 = (f32[]{:T(128)}, f32[]{:T(128)}, f32[]{:T(128)}, f32[]{:T(128)}) all-reduce(f32[]{:T(128)} %get-tuple-element.27, f32[]{:T(128)} %get-tuple-element.28, f32[]{:T(128)} %get-tuple-element.29, f32[]{:T(128)} %get-tuple-element.30), channel_id=1, replica_groups=mesh['row_0'=4,'row_1'=2,'col_0'=2,'col_1'=8,'col_2'=2] {'col_0'}, use_global_device_ids=true, to_apply=%region_15.0 | all-reduce | flops 4 | bytes 32 | tf_op jit(solution)/shard_map/psum | solution.py:20
  63.2 12.3 %all-reduce = (f32[]{:T(128)}, f32[]{:T(128)}, f32[]{:T(128)}, f32[]{:T(128)}) all-reduce(f32[]{:T(128)} %get-tuple-element.23, f32[]{:T(128)} %get-tuple-element.24, f32[]{:T(128)} %get-tuple-element.25, f32[]{:T(128)} %get-tuple-element.26), channel_id=1, replica_groups=mesh['row_0'=4,'row_1'=2,'col_0'=2,'col_1'=8,'col_2'=2] {'col_1'}, use_global_device_ids=true, to_apply=%region_16.0 | all-reduce | flops 4 | bytes 32 | tf_op jit(solution)/shard_map/psum | solution.py:20
  75.5 12.2 %all-reduce.2 = (f32[]{:T(128)}, f32[]{:T(128)}, f32[]{:T(128)}, f32[]{:T(128)}) all-reduce(f32[]{:T(128)} %get-tuple-element.11, f32[]{:T(128)} %get-tuple-element.12, f32[]{:T(128)} %get-tuple-element.13, f32[]{:T(128)} %get-tuple-element.14), channel_id=1, replica_groups=mesh['row_0'=4,'row_1'=2,'col_0'=2,'col_1'=8,'col_2'=2] {'col_2'}, use_global_device_ids=true, to_apply=%region_17.0 | all-reduce | flops 4 | bytes 32 | tf_op jit(solution)/shard_map/psum | solution.py:20
  89.0 1.0 fusion.8
  90.0 1.6 %broadcast_in_dim.8 = bf16[8,768,192]{1,2,0:T(8,128)(2,1)} broadcast(bf16[768,192]{0,1:T(8,128)(2,1)S(1)} %get-tuple-element.31), dimensions={1,2} | broadcast | bytes 2654208 | tf_op jit(solution)/shard_map/broadcast_in_dim | solution.py:27
  91.6 4.5 %all-to-all-start.2 = ((bf16[8,768,192]{1,2,0:T(8,128)(2,1)}), bf16[8,768,192]{1,2,0:T(8,128)(2,1)}, u32[]{:S(2)}, u32[]{:S(2)}) async-start(bf16[8,768,192]{1,2,0:T(8,128)(2,1)} %broadcast_in_dim.8), calls=%async_computation.2 | async-start | bytes 4718592 | tf_op jit(solution)/shard_map/all_to_all | solution.py:26
  97.4 2.0 %multiply_subtract_fusion = f32[768,768]{1,0:T(8,128)} fusion(f32[768,768]{1,0:T(8,128)S(1)} %copy-done.1, bf16[768,768]{1,0:T(8,128)(2,1)S(1)} %copy-done, f32[]{:T(128)S(6)} %max.6, f32[768]{0:T(1024)S(1)} %multiply_add_fusion, f32[768]{0:T(1024)S(1)} %get-tuple-element.34, f32[]{:T(128)S(6)} %mul.78), kind=kLoop, calls=%fused_computation.5 | loop fusion | flops 3538944 | bytes 5904392 | tf_op jit(solution)/shard_map/sub | solution.py:95
  99.4 31.4 %all-to-all-done.2 = bf16[8,768,192]{1,2,0:T(8,128)(2,1)} async-done(((bf16[8,768,192]{1,2,0:T(8,128)(2,1)}), bf16[8,768,192]{1,2,0:T(8,128)(2,1)}, u32[]{:S(2)}, u32[]{:S(2)}) %all-to-all-start.2) | async-done | bytes 2359328 | tf_op jit(solution)/shard_map/all_to_all | solution.py:26
  130.8 3.3 %copy.26 = bf16[8,24,8,768]{3,2,0,1:T(8,128)(2,1)} copy(bf16[8,24,8,768]{3,2,1,0:T(8,128)(2,1)} %bitcast) | data formatting | bytes 4718592 | tf_op jit(solution)/shard_map/reshape | solution.py:46
  (16 shorter events, 0.1 us)
Async XLA Ops:
  0.6 40.4 %copy-start.2 = (bf16[768,192]{0,1:T(8,128)(2,1)S(1)}, bf16[768,192]{0,1:T(8,128)(2,1)}, u32[]{:S(2)}) copy-start(bf16[768,192]{0,1:T(8,128)(2,1)} %param.13) | copy-start | bytes 884740
  0.6 41.3 %copy-start = (bf16[768,768]{1,0:T(8,128)(2,1)S(1)}, bf16[768,768]{1,0:T(8,128)(2,1)}, u32[]{:S(2)}) copy-start(bf16[768,768]{1,0:T(8,128)(2,1)} %param.9) | copy-start | bytes 3538948
  0.7 40.3 %copy-start.8 = (f32[768]{0:T(1024)S(1)}, f32[768]{0:T(1024)}, u32[]{:S(2)}) copy-start(f32[768]{0:T(1024)} %param.14) | copy-start | bytes 9220
  0.7 40.3 %copy-start.9 = (f32[768]{0:T(1024)S(1)}, f32[768]{0:T(1024)}, u32[]{:S(2)}) copy-start(f32[768]{0:T(1024)} %param.10) | copy-start | bytes 9220
  0.7 40.4 %copy-start.3 = (f32[768,192]{0,1:T(8,128)S(1)}, f32[768,192]{0,1:T(8,128)}, u32[]{:S(2)}) copy-start(f32[768,192]{0,1:T(8,128)} %param.12) | copy-start | bytes 1769476
  4.5 11.0 %all-to-all-start.1 = ((f32[8,1,960]{2,1,0:T(1,128)}), f32[8,1,960]{2,1,0:T(1,128)S(1)}, u32[]{:S(2)}, u32[]{:S(2)}) async-start(f32[8,1,960]{2,1,0:T(1,128)} %broadcast_in_dim.7), calls=%async_computation.1 | async-start | bytes 65536 | tf_op jit(solution)/shard_map/all_to_all | solution.py:26
  16.2 24.6 %all-to-all-start = ((f32[32,1,1536]{2,1,0:T(1,128)}), f32[32,1,1536]{2,1,0:T(1,128)S(1)}, u32[]{:S(2)}, u32[]{:S(2)}) async-start(f32[32,1,1536]{2,1,0:T(1,128)} %broadcast_in_dim.6), calls=%async_computation | async-start | bytes 393216 | tf_op jit(solution)/shard_map/all_to_all | solution.py:26
  29.9 59.1 %copy-start.7 = (f32[192]{0:T(256)}, f32[192]{0:T(256)S(1)}, u32[]{:S(2)}) copy-start(f32[192]{0:T(256)S(1)} %multiply_add_fusion.1) | copy-start | bytes 2308
  30.6 66.8 %copy-start.5 = (f32[768]{0:T(1024)}, f32[768]{0:T(1024)S(1)}, u32[]{:S(2)}) copy-start(f32[768]{0:T(1024)S(1)} %multiply_add_fusion) | copy-start | bytes 9220
  41.0 49.1 %copy-start.4 = (f32[768]{0:T(1024)}, f32[768]{0:T(1024)S(1)}, u32[]{:S(2)}) copy-start(f32[768]{0:T(1024)S(1)} %get-tuple-element.33) | copy-start | bytes 9220
  41.0 56.4 %copy-start.6 = (f32[768]{0:T(1024)}, f32[768]{0:T(1024)S(1)}, u32[]{:S(2)}) copy-start(f32[768]{0:T(1024)S(1)} %get-tuple-element.34) | copy-start | bytes 9220
  91.6 5.8 %copy-start.1 = (f32[768,768]{1,0:T(8,128)S(1)}, f32[768,768]{1,0:T(8,128)}, u32[]{:S(2)}) copy-start(f32[768,768]{1,0:T(8,128)} %param.8) | copy-start | bytes 7077892
  91.6 39.2 %all-to-all-start.2 = ((bf16[8,768,192]{1,2,0:T(8,128)(2,1)}), bf16[8,768,192]{1,2,0:T(8,128)(2,1)}, u32[]{:S(2)}, u32[]{:S(2)}) async-start(bf16[8,768,192]{1,2,0:T(8,128)(2,1)} %broadcast_in_dim.8), calls=%async_computation.2 | async-start | bytes 4718592 | tf_op jit(solution)/shard_map/all_to_all | solution.py:26
where the time goes:
time: 135 us; the launch traced here: 134 us
  waiting for transfers between devices  46.7 us (35%)
  blocking collectives  42.5 us (31%)
  starting transfers between devices  23.4 us (17%)
  other arithmetic  12 us (9%)
  local copies, waits for them, and re-layouts  6.37 us (5%)
  between operations  3.36 us (2%)
    all_to_all x3, waiting for transfers between devices, from_everyone(): lax.all_to_all(jnp.broadcast_to(value[None], (length, *value.shape)), axi...  46.7 us
    psum x5, blocking collectives, over_axes(): value = lax.psum(value, axis)  42.5 us
    all_to_all x3, starting transfers between devices, from_everyone(): lax.all_to_all(jnp.broadcast_to(value[None], (length, *value.shape)), axi...  23.4 us
    reduce_sum x2, other arithmetic, local(): clip_local = (jnp.sum(jnp.square(mlp_raw)), jnp.sum(jnp.square(attn_raw)))  4.2 us
    reshape x1, local copies, waits for them, and re-layouts, in_order(): pieces.reshape(*dims[:dim], dims[dim] * dims[dim + 1], *dims[dim + 2:])  3.35 us
    broadcast_in_dim x3, local copies, waits for them, and re-layouts, from_everyone(): jnp.broadcast_to(value[None], (length, *value.shape))  2.97 us
  transfers between devices with their start and end apart: 3, of which 3 were waited for; matrix products, arithmetic and copies ran while one was open for 3% of the time, Pallas kernels for 0%

commit v1 on v0

v1 whole, which is shorter than its diff:
```python
import jax
import jax.numpy as jnp
from jax import lax
from jax.sharding import Mesh
from jax.sharding import PartitionSpec as P

STEP = 4
ROW = ("row_0", "row_1")
COL = ("col_0", "col_1", "col_2")
Y_HI, Z, CORE = COL
PLANE = (Y_HI, "row_0", "row_1")

TINY_SQUARE = 1e-30
LEARN_RATE = 0.05
DECAY_POWER = 0.8


def from_everyone(value, axes):
    length = lax.axis_size(axes)
    return lax.all_to_all(
        jnp.broadcast_to(value[None], (length, *value.shape)), axes, 0, 0, tiled=True
    )


def other_core(value):
    return lax.ppermute(value, CORE, [(0, 1), (1, 0)])


def local(
    mlp_param,
    mlp_grad,
    mlp_row_state,
    mlp_col_state,
    attn_param,
    attn_grad,
    attn_row_state,
    attn_col_state,
):
    keep = 1.0 - STEP ** (-DECAY_POWER)
    rows, mlp_cols = mlp_grad.shape
    attn_cols = attn_grad.shape[1]
    half = rows // 2
    row_devices = lax.axis_size(ROW)
    rows_total = rows * row_devices
    mlp_width = mlp_cols * lax.axis_size(COL)
    attn_width = attn_cols * lax.axis_size(COL)
    mlp_count = float(rows_total * mlp_width)
    attn_count = float(rows_total * attn_width)
    y_hi = lax.axis_index(Y_HI)
    row = lax.axis_index(ROW)
    core = lax.axis_index(CORE)
    attn_grad, attn_param = attn_grad.T, attn_param.T

    mlp_g2 = jnp.square(mlp_grad.astype(jnp.float32))
    attn_g2 = jnp.square(attn_grad.astype(jnp.float32))
    mlp_square, attn_square = mlp_g2 + TINY_SQUARE, attn_g2 + TINY_SQUARE
    row_sums = jnp.concatenate([jnp.sum(mlp_square, axis=1), jnp.sum(attn_square, axis=0)])
    col_sums = jnp.concatenate([jnp.sum(mlp_square, axis=0), jnp.sum(attn_square, axis=1)])
    col_sums = jnp.pad(col_sums, (0, 2 * rows - col_sums.size))
    p_mlp, p_attn = jnp.sum(jnp.square(mlp_param)), jnp.sum(jnp.square(attn_param))

    same = jnp.arange(2)[:, None, None] == y_hi
    sent = jnp.where(same, col_sums, row_sums)
    sent = jnp.broadcast_to(sent, (2, row_devices, 2 * rows)).reshape(2 * row_devices, 2 * rows)
    got = lax.all_to_all(sent, PLANE, 0, 0, tiled=True)
    place = jnp.arange(2 * row_devices)[:, None]
    col_total = jnp.sum(jnp.where(place // row_devices == y_hi, got, 0.0), axis=0)
    from_partner = place == (1 - y_hi) * row_devices + row
    row_sums = row_sums + jnp.sum(jnp.where(from_partner, got, 0.0), axis=0)
    mlp_cols_new = keep * mlp_col_state + (1.0 - keep) * (col_total[:mlp_cols] / rows_total)
    attn_cols_new = keep * attn_col_state + (1.0 - keep) * (
        col_total[mlp_cols : mlp_cols + attn_cols] / rows_total
    )

    w_mlp = jnp.sum(mlp_g2 * (1.0 / mlp_cols_new)[None, :], axis=1)
    w_attn = jnp.sum(attn_g2 * (1.0 / attn_cols_new)[:, None], axis=0)
    p_sums = jnp.pad(jnp.stack([p_mlp, p_attn]), (0, 126))
    packed = jnp.concatenate([row_sums, w_mlp, w_attn, p_sums])
    packed = packed + other_core(packed)
    mine = lax.dynamic_index_in_dim(packed[: 4 * rows].reshape(4, 2, half), core, 1, keepdims=False)
    mine = jnp.concatenate([mine.reshape(-1), packed[4 * rows :]])
    mine = from_everyone(mine, Z).sum(axis=0)
    r_mlp, r_attn, w_mlp, w_attn = mine[: 4 * half].reshape(4, half)
    p_mlp, p_attn = mine[4 * half], mine[4 * half + 1]
    mlp_state = lax.dynamic_index_in_dim(mlp_row_state.reshape(2, half), core, 0, keepdims=False)
    attn_state = lax.dynamic_index_in_dim(attn_row_state.reshape(2, half), core, 0, keepdims=False)
    mlp_half = keep * mlp_state + (1.0 - keep) * (r_mlp / mlp_width)
    attn_half = keep * attn_state + (1.0 - keep) * (r_attn / attn_width)
    q_sums = jnp.stack([jnp.sum(w_mlp / mlp_half), jnp.sum(w_attn / attn_half)])

    sent = jnp.concatenate([mlp_half, attn_half, jnp.pad(q_sums, (0, 126))])
    got = other_core(sent)
    first, last = jnp.where(core == 0, sent, got), jnp.where(core == 0, got, sent)
    mlp_rows_new = jnp.concatenate([first[:half], last[:half]])
    attn_rows_new = jnp.concatenate([first[half : 2 * half], last[half : 2 * half]])
    q_sums = q_sums + got[2 * half : 2 * half + 2]

    totals = jnp.concatenate([q_sums, jnp.stack([p_mlp, p_attn]), jnp.zeros((124,), jnp.float32)])
    totals = from_everyone(totals, PLANE).sum(axis=0)
    mlp_clip = jnp.maximum(1.0, jnp.sqrt(totals[0] / mlp_count))
    attn_clip = jnp.maximum(1.0, jnp.sqrt(totals[1] / attn_count))
    mlp_step = LEARN_RATE * jnp.sqrt(totals[2] / mlp_count)
    attn_step = LEARN_RATE * jnp.sqrt(totals[3] / attn_count)

    attn_scale = (attn_step / attn_clip) * lax.rsqrt(attn_cols_new)
    attn_new = attn_param - attn_grad.astype(jnp.float32) * attn_scale[:, None] * lax.rsqrt(attn_rows_new)[None, :]
    mlp_scale = (mlp_step / mlp_clip) * lax.rsqrt(mlp_rows_new)
    mlp_new = mlp_param - mlp_grad.astype(jnp.float32) * mlp_scale[:, None] * lax.rsqrt(mlp_cols_new)[None, :]
    block, mlp_new = lax.optimization_barrier((attn_new.astype(jnp.bfloat16), mlp_new))
    copy = from_everyone(block, ROW)
    copy = jnp.moveaxis(copy, 0, 1).reshape(attn_cols, rows_total).T
    return (
        mlp_new,
        attn_new.T,
        mlp_rows_new,
        mlp_cols_new,
        attn_rows_new,
        attn_cols_new,
        copy,
    )


def solution(mesh):
    finer = Mesh(mesh.devices.reshape(4, 2, 2, 8, 2), (*ROW, *COL))
    return jax.shard_map(
        local,
        mesh=finer,
        in_specs=(
            P(ROW, COL),
            P(ROW, COL),
            P(ROW),
            P(COL),
            P(ROW, COL),
            P(ROW, COL),
            P(ROW),
            P(COL),
        ),
        out_specs=(P(ROW, COL), P(ROW, COL), P(ROW), P(COL), P(ROW), P(COL), P(None, COL)),
        check_vma=False,
    )
```

time: 135 us -> 116 us (0.86)
  waiting for transfers between devices: 46.7 us -> 14.4 us
  other arithmetic: 12 us -> 31.3 us
  blocking collectives: 42.5 us -> 30 us
  local copies, waits for them, and re-layouts: 6.37 us -> 11 us
    psum x5 -> x0, blocking collectives: 42.5 us -> none  [over_axes(): value = lax.psum(value, axis)]
    all_to_all x3, waiting for transfers between devices: 46.7 us -> 12.1 us  [the longest x2 10.3 us: from_everyone(): lax.all_to_all(jnp.broadcast_to(value[None], (length, *value.shape)), axe...]
    all_to_all x0 -> x1, blocking collectives: none -> 30 us  [from_everyone(): lax.all_to_all(jnp.broadcast_to(value[None], (length, *value.shape)), axe...]
    ppermute x0 -> x2, starting transfers between devices: none -> 3.75 us  [other_core(): return lax.ppermute(value, CORE, [(0, 1), (1, 0)])]
    all_to_all x3, starting transfers between devices: 23.4 us -> 19.9 us  [the longest x2 12.2 us: from_everyone(): lax.all_to_all(jnp.broadcast_to(value[None], (length, *value.shape)), axe...]
    reduce_sum x5 -> x9, other arithmetic: 6.18 us -> 9.6 us  [the longest x1 1.91 us: local(): jnp.sum(mlp_square, axis=0)]
    another operation x0 -> x2, other arithmetic: none -> 3.23 us  [the longest x1 1.88 us: local(): p_sums = jnp.pad(jnp.stack([p_mlp, p_attn]), (0, 126))]
    concatenate x2 -> x5, other arithmetic: 0.01 us -> 2.62 us  [the longest x1 1.27 us: local(): packed = jnp.concatenate([row_sums, w_mlp, w_attn, p_sums])]
  transfers between devices with their start and end apart: 3 -> 5, of which waited for: 3 -> 5; matrix products, arithmetic and copies ran while one was open for 3% -> 7% of each run, Pallas kernels for 0% -> 0%
where the time goes in v1:
time: 116 us; the launch traced here: 114 us
  other arithmetic  31.3 us (27%)
  blocking collectives  30 us (26%)
  starting transfers between devices  23.6 us (20%)
  waiting for transfers between devices  14.4 us (12%)
  local copies, waits for them, and re-layouts  11 us (9%)
  between operations  3.64 us (3%)
    all_to_all x1, blocking collectives, from_everyone(): lax.all_to_all(jnp.broadcast_to(value[None], (length, *value.shape)), axe...  30 us
    all_to_all x2, starting transfers between devices, from_everyone(): lax.all_to_all(jnp.broadcast_to(value[None], (length, *value.shape)), axe...  12.2 us
    all_to_all x2, waiting for transfers between devices, from_everyone(): lax.all_to_all(jnp.broadcast_to(value[None], (length, *value.shape)), axe...  10.3 us
    all_to_all x1, starting transfers between devices, local(): got = lax.all_to_all(sent, PLANE, 0, 0, tiled=True)  7.62 us
    ppermute x2, starting transfers between devices, other_core(): return lax.ppermute(value, CORE, [(0, 1), (1, 0)])  3.75 us
    sub x1, other arithmetic, local(): mlp_param - mlp_grad.astype(jnp.float32) * mlp_scale[:, None] * lax.rsqrt...  2.46 us
    ppermute x2, waiting for transfers between devices, other_core(): return lax.ppermute(value, CORE, [(0, 1), (1, 0)])  2.34 us
  transfers between devices with their start and end apart: 5, of which 5 were waited for; matrix products, arithmetic and copies ran while one was open for 7% of the time, Pallas kernels for 0%

profile of v1, /device:TPU:1, one launch (start us, length us, event | category | flops | bytes accessed | tf_op | source)
XLA Modules:
  0.0 114.0 jit_solution(2232622674434442473)
XLA Ops:
  0.7 1.3 %fusion.9 = (f32[192]{0:T(256)S(1)}, f32[768]{0:T(1024)S(1)}) fusion(bf16[768,192]{0,1:T(8,128)(2,1)} %param.13), kind=kLoop, calls=%fused_computation.14 | loop fusion | flops 736320 | bytes 298752 | tf_op jit(solution)/shard_map/reduce_sum | solution.py:58
  2.0 1.9 %fusion.2 = (f32[768]{0:T(1024)S(1)}, f32[768]{0:T(1024)S(1)}) fusion(bf16[768,768]{1,0:T(8,128)(2,1)} %param.9), kind=kLoop, calls=%fused_computation.4 | loop fusion | flops 2947584 | bytes 1185792 | tf_op jit(solution)/shard_map/reduce_sum | solution.py:58
  4.6 1.6 %all_to_all.19 = f32[16,1,1536]{2,1,0:T(1,128)} reshape(f32[2,8,1536]{2,1,0:T(8,128)} %broadcast_in_dim.72) | data formatting | bytes 196608 | tf_op jit(solution)/shard_map/all_to_all | solution.py:65
  6.3 7.6 %all-to-all-start = ((f32[16,1,1536]{2,1,0:T(1,128)}), f32[16,1,1536]{2,1,0:T(1,128)}, u32[]{:S(2)}, u32[]{:S(2)}) async-start(f32[16,1,1536]{2,1,0:T(1,128)} %all_to_all.19), calls=%async_computation | async-start | bytes 196608 | tf_op jit(solution)/shard_map/all_to_all | solution.py:65
  13.9 1.8 %multiply_reduce_fusion.1 = f32[]{:T(128)} fusion(f32[768,192]{0,1:T(8,128)} %param.12), kind=kLoop, calls=%fused_computation.19 | loop fusion | flops 294911 | bytes 589828 | tf_op jit(solution)/shard_map/reduce_sum | solution.py:60
  15.7 1.2 %multiply_reduce_fusion = f32[]{:T(128)} fusion(f32[768,768]{1,0:T(8,128)S(1)} %copy-done.1), kind=kLoop, calls=%fused_computation.9 | loop fusion | flops 1179647 | bytes 2359300 | tf_op jit(solution)/shard_map/reduce_sum | solution.py:60
  16.9 1.9 %fusion.23 = f32[128]{0:T(128)} fusion(f32[1]{0:T(128)} %bitcast.1, f32[1]{0:T(128)} %bitcast), kind=kLoop, calls=%fused_computation.62 | loop fusion | flops 512 | bytes 520 | tf_op jit(solution)/shard_map/stack | solution.py:77
  18.8 1.8 %all-to-all-done = f32[16,1,1536]{2,1,0:T(1,128)} async-done(((f32[16,1,1536]{2,1,0:T(1,128)}), f32[16,1,1536]{2,1,0:T(1,128)}, u32[]{:S(2)}, u32[]{:S(2)}) %all-to-all-start) | async-done | bytes 98336 | tf_op jit(solution)/shard_map/all_to_all | solution.py:65
  20.6 1.0 fusion.14
  21.7 1.2 %broadcast_divide_fusion.1 = (f32[192]{0:T(256)S(1)}, f32[192]{0:T(256)}) fusion(f32[1536]{0:T(1024)S(1)} %get-tuple-element.16, f32[192]{0:T(256)} %param.15), kind=kLoop, calls=%fused_computation.66 | loop fusion | flops 768 | bytes 3072 | tf_op jit(solution)/shard_map/div | solution.py:76
  22.9 1.3 %fusion.25 = (f32[768]{0:T(1024)}, f32[768]{0:T(1024)S(1)}) fusion(f32[1536]{0:T(1024)S(1)} %get-tuple-element.16, f32[768]{0:T(1024)} %param.11), kind=kLoop, calls=%fused_computation.70 | loop fusion | flops 2304 | bytes 12288 | tf_op jit(solution)/shard_map/rsqrt | solution.py:108
  24.2 1.1 fusion.11
  25.7 1.3 %pad_maximum_fusion = f32[3200]{0:T(1024)} fusion(f32[128]{0:T(128)} %fusion.23, f32[768]{0:T(1024)S(1)} %fusion.11, f32[768]{0:T(1024)S(1)} %fusion.4, f32[1536]{0:T(1024)S(1)} %fusion.24), kind=kLoop, calls=%fused_computation.25 | loop fusion | flops 9600 | bytes 25600 | tf_op jit(solution)/shard_map/concatenate | solution.py:78
  27.0 2.0 %collective-permute-start = (f32[3200]{0:T(1024)}, f32[3200]{0:T(1024)}, u32[]{:S(2)}, u32[]{:S(2)}) collective-permute-start(f32[3200]{0:T(1024)} %pad_maximum_fusion), channel_id=1, source_target_pairs={{0,1},{1,0},{2,3},{3,2},{4,5},{5,4},{6,7},{7,6},{8,9},{9,8},{10,11... | collective-permute-start | bytes 38408 | tf_op jit(solution)/shard_map/ppermute | solution.py:26
  28.9 1.2 %collective-permute-done = f32[3200]{0:T(1024)} collective-permute-done((f32[3200]{0:T(1024)}, f32[3200]{0:T(1024)}, u32[]{:S(2)}, u32[]{:S(2)}) %collective-permute-start) | collective-permute-done | bytes 12832 | tf_op jit(solution)/shard_map/ppermute | solution.py:26
  32.0 0.7 dynamic-slice_reduce_fusion
  34.0 8.2 %all-to-all-start.1 = ((f32[8,1,1664]{2,1,0:T(1,128)}), f32[8,1,1664]{2,1,0:T(1,128)}, u32[]{:S(2)}, u32[]{:S(2)}) async-start(f32[8,1,1664]{2,1,0:T(1,128)} %broadcast_in_dim.75), calls=%async_computation.1 | async-start | bytes 106496 | tf_op jit(solution)/shard_map/all_to_all | solution.py:20
  44.2 5.2 %all-to-all-done.1 = f32[8,1,1664]{2,1,0:T(1,128)} async-done(((f32[8,1,1664]{2,1,0:T(1,128)}), f32[8,1,1664]{2,1,0:T(1,128)}, u32[]{:S(2)}, u32[]{:S(2)}) %all-to-all-start.1) | async-done | bytes 53280 | tf_op jit(solution)/shard_map/all_to_all | solution.py:20
  49.4 0.9 reduce_sum.136
  50.3 1.3 %fusion.19 = (f32[]{:T(128)}, f32[]{:T(128)}, f32[384]{0:T(512)S(1)}, f32[384]{0:T(512)S(1)}) fusion(f32[1664]{0:T(1024)S(1)} %reduce_sum.136, f32[384]{0:T(512)} %get-tuple-element.45, f32[384]{0:T(512)} %get-tuple-element.46), kind=kLoop, calls=%fused_computation.46 | loop fusion | flops 3070 | bytes 12296 | tf_op jit(solution)/shard_map/reduce_sum | solution.py:89
  51.6 1.4 %pad_maximum_fusion.5 = f32[2]{0:T(128)S(1)} fusion(f32[1]{0:T(128)} %bitcast.3, f32[1]{0:T(128)} %bitcast.2), kind=kLoop, calls=%fused_computation.63 | loop fusion | flops 2 | bytes 16 | tf_op jit(solution)/shard_map/stack | solution.py:89
  54.1 1.8 %collective-permute-start.1 = (f32[896]{0:T(1024)}, f32[896]{0:T(1024)}, u32[]{:S(2)}, u32[]{:S(2)}) collective-permute-start(f32[896]{0:T(1024)} %select_maximum_fusion.1), channel_id=1, source_target_pairs={{0,1},{1,0},{2,3},{3,2},{4,5},{5,4},{6,7},{7,6},{8,9},{9,8},{10,11... | collective-permute-start | bytes 10760 | tf_op jit(solution)/shard_map/ppermute | solution.py:26
  55.9 1.2 %collective-permute-done.1 = f32[896]{0:T(1024)} collective-permute-done((f32[896]{0:T(1024)}, f32[896]{0:T(1024)}, u32[]{:S(2)}, u32[]{:S(2)}) %collective-permute-start.1) | collective-permute-done | bytes 3616 | tf_op jit(solution)/shard_map/ppermute | solution.py:26
  58.9 2.0 %slice_add_fusion = f32[2]{0:T(128)S(1)} fusion(f32[896]{0:T(1024)} %collective-permute-done.1, f32[1]{0:T(128)} %bitcast.3, f32[1]{0:T(128)} %bitcast.2), kind=kLoop, calls=%fused_computation.65 | loop fusion | flops 4 | bytes 24 | tf_op jit(solution)/shard_map/add | solution.py:96
  61.6 4.1 %all-to-all-start.2 = ((f32[16,1,128]{2,1,0:T(1,128)}), f32[16,1,128]{2,1,0:T(1,128)S(1)}, u32[]{:S(2)}, u32[]{:S(2)}) async-start(f32[16,1,128]{2,1,0:T(1,128)} %broadcast_in_dim.77), calls=%async_computation.2 | async-start | bytes 16384 | tf_op jit(solution)/shard_map/all_to_all | solution.py:20
  65.7 1.3 %fusion.28 = (f32[768]{0:T(1024)S(1)}, f32[768]{0:T(1024)}) fusion(f32[384]{0:T(512)} %get-tuple-element.36, f32[384]{0:T(512)S(1)} %get-tuple-element.34), kind=kLoop, calls=%fused_computation.71 | loop fusion | flops 768 | bytes 9216 | tf_op jit(solution)/shard_map/rsqrt | solution.py:106
  67.0 5.1 %all-to-all-done.2 = f32[16,1,128]{2,1,0:T(1,128)S(1)} async-done(((f32[16,1,128]{2,1,0:T(1,128)}), f32[16,1,128]{2,1,0:T(1,128)S(1)}, u32[]{:S(2)}, u32[]{:S(2)}) %all-to-all-start.2) | async-done | bytes 8224 | tf_op jit(solution)/shard_map/all_to_all | solution.py:20
  76.3 2.1 %convert_bitcast_fusion = (bf16[192,768]{1,0:T(8,128)(2,1)S(1)}, f32[768,192]{0,1:T(8,128)}) fusion(f32[768,192]{0,1:T(8,128)} %param.12, f32[768]{0:T(1024)S(1)} %get-tuple-element.25, f32[192]{0:T(256)S(1)} %rsqrt_multiply_fusion.1, bf16[768,192]{0,1:T(8,128)(2,1)} %param.13), kind=kLoop, calls=%fused_computation.20 | loop fusion | flops 737280 | bytes 1773312 | tf_op jit(solution)/shard_map/sub | solution.py:106
  78.4 1.3 %rsqrt_multiply_fusion = (f32[768]{0:T(1024)S(1)}, f32[768]{0:T(1024)}) fusion(f32[]{:T(128)} %bitcast.7, f32[384]{0:T(512)} %get-tuple-element.35, f32[384]{0:T(512)} %get-tuple-element.33), kind=kLoop, calls=%fused_computation.38 | loop fusion | flops 1536 | bytes 9220 | tf_op jit(solution)/shard_map/mul | solution.py:107
  79.7 2.5 %fusion.6 = f32[768,768]{1,0:T(8,128)} fusion(f32[768,768]{1,0:T(8,128)S(1)} %copy-done.1, bf16[768,768]{1,0:T(8,128)(2,1)S(1)} %copy-done, f32[768]{0:T(1024)} %get-tuple-element.21, f32[768]{0:T(1024)S(1)} %get-tuple-element.19), kind=kLoop, calls=%fused_computation.8 | loop fusion | flops 2359296 | bytes 5904384 | tf_op jit(solution)/shard_map/sub | solution.py:108
  82.3 30.0 %all_to_all.29 = bf16[8,192,768]{2,1,0:T(8,128)(2,1)S(1)} all-to-all(bf16[8,192,768]{2,1,0:T(8,128)(2,1)S(1)} %broadcast_in_dim.78), channel_id=1, replica_groups=mesh['row_0'=4,'row_1'=2,'col_0'=2,'col_1'=8,'col_2'=2] {'row_0','row_1'}, dimensions={0} | all-to-all | bytes 4718592 | tf_op jit(solution)/shard_map/all_to_all | solution.py:20
  112.3 1.7 %copy.27 = bf16[8,24,8,768]{3,2,0,1:T(8,128)(2,1)} copy(bf16[8,24,8,768]{3,2,1,0:T(8,128)(2,1)S(1)} %bitcast.21) | data formatting | bytes 4718592 | tf_op jit(solution)/shard_map/reshape | solution.py:111
  (38 shorter events, 11.5 us)
Async XLA Ops:
  0.6 15.1 %copy-start.1 = (f32[768,768]{1,0:T(8,128)S(1)}, f32[768,768]{1,0:T(8,128)}, u32[]{:S(2)}) copy-start(f32[768,768]{1,0:T(8,128)} %param.8) | copy-start | bytes 7077892
  2.0 23.3 %copy-start = (bf16[768,768]{1,0:T(8,128)(2,1)S(1)}, bf16[768,768]{1,0:T(8,128)(2,1)}, u32[]{:S(2)}) copy-start(bf16[768,768]{1,0:T(8,128)(2,1)} %param.9) | copy-start | bytes 3538948
  6.3 14.4 %all-to-all-start = ((f32[16,1,1536]{2,1,0:T(1,128)}), f32[16,1,1536]{2,1,0:T(1,128)}, u32[]{:S(2)}, u32[]{:S(2)}) async-start(f32[16,1,1536]{2,1,0:T(1,128)} %all_to_all.19), calls=%async_computation | async-start | bytes 196608 | tf_op jit(solution)/shard_map/all_to_all | solution.py:65
  24.2 1.1 copy-start.2
  27.0 3.2 %collective-permute-start = (f32[3200]{0:T(1024)}, f32[3200]{0:T(1024)}, u32[]{:S(2)}, u32[]{:S(2)}) collective-permute-start(f32[3200]{0:T(1024)} %pad_maximum_fusion), channel_id=1, source_target_pairs={{0,1},{1,0},{2,3},{3,2},{4,5},{5,4},{6,7},{7,6},{8,9},{9,8},{10,11... | collective-permute-start | bytes 38408 | tf_op jit(solution)/shard_map/ppermute | solution.py:26
  34.0 15.4 %all-to-all-start.1 = ((f32[8,1,1664]{2,1,0:T(1,128)}), f32[8,1,1664]{2,1,0:T(1,128)}, u32[]{:S(2)}, u32[]{:S(2)}) async-start(f32[8,1,1664]{2,1,0:T(1,128)} %broadcast_in_dim.75), calls=%async_computation.1 | async-start | bytes 106496 | tf_op jit(solution)/shard_map/all_to_all | solution.py:20
  53.0 0.5 copy-start.3
  54.1 2.9 %collective-permute-start.1 = (f32[896]{0:T(1024)}, f32[896]{0:T(1024)}, u32[]{:S(2)}, u32[]{:S(2)}) collective-permute-start(f32[896]{0:T(1024)} %select_maximum_fusion.1), channel_id=1, source_target_pairs={{0,1},{1,0},{2,3},{3,2},{4,5},{5,4},{6,7},{7,6},{8,9},{9,8},{10,11... | collective-permute-start | bytes 10760 | tf_op jit(solution)/shard_map/ppermute | solution.py:26
  61.6 10.4 %all-to-all-start.2 = ((f32[16,1,128]{2,1,0:T(1,128)}), f32[16,1,128]{2,1,0:T(1,128)S(1)}, u32[]{:S(2)}, u32[]{:S(2)}) async-start(f32[16,1,128]{2,1,0:T(1,128)} %broadcast_in_dim.77), calls=%async_computation.2 | async-start | bytes 16384 | tf_op jit(solution)/shard_map/all_to_all | solution.py:20

commit v2 on v0

v2 whole, which is shorter than its diff:
```python
import functools

import jax
import jax.numpy as jnp
from jax import lax
from jax.experimental import pallas as pl
from jax.experimental.pallas import tpu as pltpu
from jax.sharding import Mesh
from jax.sharding import PartitionSpec as P

STEP = 4
ROW = ("row_0", "row_1")
COL = ("col_0", "col_1", "col_2")
Y_HI, Z, CORE = COL
PLANE = (Y_HI, "row_0", "row_1")

TINY_SQUARE = 1e-30
LEARN_RATE = 0.05
DECAY_POWER = 0.8
KEEP = 1.0 - STEP ** (-DECAY_POWER)

F32, BF16 = jnp.float32, jnp.bfloat16
SLAB = 16
LANES = 128
ON_CHIP = pl.BlockSpec(memory_space=pltpu.VMEM)
OFF_CHIP = pl.BlockSpec(memory_space=pltpu.HBM)


def call(kernel, outs, args, in_specs=None, out_specs=None, scratch=(), limit=4 << 20):
    return pl.pallas_call(
        kernel,
        out_shape=outs,
        in_specs=in_specs or [ON_CHIP] * len(args),
        out_specs=out_specs or [ON_CHIP] * len(outs),
        scratch_shapes=scratch,
        compiler_params=pltpu.CompilerParams(vmem_limit_bytes=limit),
    )(*args)


def tiles(value):
    width = value.shape[1] // LANES
    return sum((value[:, k * LANES : (k + 1) * LANES] for k in range(1, width)), value[:, :LANES])


def wide(value, width):
    return jnp.concatenate([value] * (width // LANES), axis=1)


def turned_sum(ref, start):
    return jnp.sum(ref[pl.ds(start, LANES), :].T, axis=0, keepdims=True)


def down(value):
    return jnp.broadcast_to(value, (LANES, LANES)).T


def fold(value):
    return value[:8] + value[8:]


def sums_kernel(
    g_hbm, ga_hbm, p_hbm, pa_hbm, sent_ref, rows_ref, psum_ref, g_ref, ga_ref, p_ref, pa_ref, lane_ref, acc_ref, sems
):
    rows, cols = g_hbm.shape
    attn_cols = ga_hbm.shape[0]
    blocks = rows // LANES
    g_copies = [
        pltpu.make_async_copy(g_hbm.at[pl.ds(b * LANES, LANES)], g_ref.at[pl.ds(b * LANES, LANES)], sems.at[b])
        for b in range(blocks)
    ]
    p_copies = [
        pltpu.make_async_copy(
            p_hbm.at[pl.ds(b * LANES, LANES)], p_ref.at[pl.ds(b * LANES, LANES)], sems.at[blocks + b]
        )
        for b in range(blocks)
    ]
    ga_copy = pltpu.make_async_copy(ga_hbm, ga_ref, sems.at[2 * blocks])
    pa_copy = pltpu.make_async_copy(pa_hbm, pa_ref, sems.at[2 * blocks + 1])
    for copy in (*g_copies, ga_copy, *p_copies, pa_copy):
        copy.start()
    acc_ref[...] = jnp.zeros_like(acc_ref)
    lane_ref[pl.ds(rows, 2 * LANES), :] = jnp.zeros((2 * LANES, LANES), F32)

    def squares(ref, start, first):
        def step(s, acc):
            g = ref[pl.ds(start + s * SLAB, SLAB), :].astype(F32)
            g = g * g
            lane_ref[pl.ds(first + start + s * SLAB, SLAB), :] = tiles(g)
            return acc + fold(g)

        return step

    def own_squares(ref, start):
        def step(s, acc):
            p = ref[pl.ds(start + s * SLAB, SLAB), :]
            return acc + fold(p * p)

        return step

    eight = jnp.zeros((8, cols), F32)
    steps = LANES // SLAB
    col_sum = eight
    for b, copy in enumerate(g_copies):
        copy.wait()
        col_sum = lax.fori_loop(0, steps, squares(g_ref, b * LANES, 0), col_sum, unroll=True)
        rows_ref[:, pl.ds(b * LANES, LANES)] = turned_sum(lane_ref, b * LANES)
    ga_copy.wait()
    row_sum = lax.fori_loop(0, attn_cols // SLAB, squares(ga_ref, 0, rows), jnp.zeros((8, rows), F32), unroll=4)
    rows_ref[:, pl.ds(rows, rows)] = jnp.sum(row_sum, axis=0, keepdims=True)
    rows_ref[...] += jnp.concatenate(
        [jnp.full((1, rows), cols * TINY_SQUARE, F32), jnp.full((1, rows), attn_cols * TINY_SQUARE, F32)], axis=1
    )
    col_sums = jnp.concatenate(
        [
            jnp.sum(col_sum, axis=0, keepdims=True),
            turned_sum(lane_ref, rows),
            turned_sum(lane_ref, rows + LANES),
        ],
        axis=1,
    ) + rows * TINY_SQUARE
    col_sums = jnp.concatenate([col_sums, jnp.zeros((1, 2 * rows - col_sums.shape[1]), F32)], axis=1)
    y_hi = lax.axis_index(Y_HI)
    devices = sent_ref.shape[0] // 2
    row_sums = rows_ref[...]
    for part in range(2):
        value = jnp.where(y_hi == part, col_sums, row_sums)
        for k in range(devices):
            sent_ref[part * devices + k] = value
    p_sum = eight
    for b, copy in enumerate(p_copies):
        copy.wait()
        p_sum = lax.fori_loop(0, steps, own_squares(p_ref, b * LANES), p_sum, unroll=True)
    pa_copy.wait()
    pa_sum = lax.fori_loop(0, attn_cols // SLAB, own_squares(pa_ref, 0), jnp.zeros((8, rows), F32), unroll=4)
    psum_ref[:, :LANES] = jnp.sum(tiles(p_sum), axis=0, keepdims=True)
    psum_ref[:, LANES:] = jnp.sum(tiles(pa_sum), axis=0, keepdims=True)


def columns_kernel(
    rows_total, got_ref, rows_ref, psum_ref, g_ref, ga_ref, state_ref, attn_state_ref,
    cols_ref, attn_cols_ref, kept_ref, sent_ref, lane_ref,
):
    rows, cols = g_ref.shape
    attn_cols = ga_ref.shape[0]
    half = rows // 2
    devices = got_ref.shape[0] // 2
    y_hi, core = lax.axis_index(Y_HI), lax.axis_index(CORE)
    row = lax.axis_index("row_0") * lax.axis_size("row_1") + lax.axis_index("row_1")
    total = got_ref[y_hi * devices]
    for k in range(1, devices):
        total = total + got_ref[y_hi * devices + k]
    row_sums = rows_ref[...] + got_ref[(1 - y_hi) * devices + row]
    cols_new = KEEP * state_ref[...].reshape(1, cols) + (1.0 - KEEP) * (total[:, :cols] / rows_total)
    cols_ref[...] = cols_new.reshape(cols)
    attn_state = attn_state_ref[...].reshape(1, attn_cols)
    attn_new = KEEP * attn_state + (1.0 - KEEP) * (total[:, cols : cols + attn_cols] / rows_total)
    attn_cols_ref[...] = attn_new.reshape(attn_cols)
    inverse = jnp.broadcast_to(1.0 / cols_new, (SLAB, cols))
    attn_inverse = jnp.concatenate([1.0 / attn_new, jnp.ones((1, 2 * LANES - attn_cols), F32)], axis=1)
    down_inverse = [down(attn_inverse[:, k * LANES : (k + 1) * LANES]) for k in range(2)]

    def step(s, carry):
        g = g_ref[pl.ds(s * SLAB, SLAB), :].astype(F32)
        lane_ref[pl.ds(s * SLAB, SLAB), :] = tiles(g * g * inverse)
        return carry

    lax.fori_loop(0, rows // SLAB, step, 0, unroll=8)
    w_attn = jnp.zeros((8, rows), F32)
    for s in range(attn_cols // SLAB):
        g = ga_ref[pl.ds(s * SLAB, SLAB), :].astype(F32)
        at = s * SLAB
        scale = down_inverse[at // LANES][at % LANES : at % LANES + SLAB]
        w_attn = w_attn + fold(g * g * wide(scale, rows))
    w_attn = jnp.sum(w_attn, axis=0, keepdims=True)
    w_mlp = jnp.concatenate([turned_sum(lane_ref, b * LANES) for b in range(rows // LANES)], axis=1)
    p_sums = psum_ref[...]
    vectors = (row_sums[:, :rows], row_sums[:, rows:], w_mlp, w_attn)
    first = jnp.concatenate([v[:, :half] for v in vectors] + [p_sums], axis=1)
    last = jnp.concatenate([v[:, half:] for v in vectors] + [p_sums], axis=1)
    kept_ref[...] = jnp.where(core == 0, first, last)
    sent_ref[...] = jnp.where(core == 0, last, first)


def spread_kernel(kept_ref, got_ref, sent_ref):
    value = kept_ref[...] + got_ref[...]
    for k in range(sent_ref.shape[0]):
        sent_ref[k] = value


def rows_kernel(widths, got_ref, state_ref, attn_state_ref, sent_ref, psum_ref):
    rows = state_ref.shape[0]
    half = rows // 2
    core = lax.axis_index(CORE)
    total = got_ref[0]
    for k in range(1, got_ref.shape[0]):
        total = total + got_ref[k]
    psum_ref[...] = total[:, 4 * half :]
    for k, (ref, width) in enumerate(zip((state_ref, attn_state_ref), widths)):
        state = ref[...].reshape(1, rows)
        state = jnp.where(core == 0, state[:, :half], state[:, half:])
        new = KEEP * state + (1.0 - KEEP) * (total[:, k * half : (k + 1) * half] / width)
        sent_ref[:, k * half : (k + 1) * half] = new
        part = total[:, (2 + k) * half : (3 + k) * half] / new
        sent_ref[:, 2 * half + k * LANES : 2 * half + (k + 1) * LANES] = tiles(part)


def scalars_kernel(own_ref, got_ref, psum_ref, rows_ref, attn_rows_ref, sent_ref):
    rows = rows_ref.shape[0]
    half = rows // 2
    core = lax.axis_index(CORE)
    own, got = own_ref[...], got_ref[...]
    first, last = jnp.where(core == 0, own, got), jnp.where(core == 0, got, own)
    rows_ref[...] = jnp.concatenate([first[:, :half], last[:, :half]], axis=1).reshape(rows)
    attn_rows_ref[...] = jnp.concatenate([first[:, half : 2 * half], last[:, half : 2 * half]], axis=1).reshape(rows)
    value = jnp.concatenate([first[:, 2 * half :] + last[:, 2 * half :], psum_ref[...]], axis=1)
    for k in range(sent_ref.shape[0]):
        sent_ref[k] = value


def update_kernel(
    counts, got_ref, rows_ref, attn_rows_ref, cols_ref, attn_cols_ref, g_ref, ga_ref, p_ref, pa_ref,
    new_hbm, attn_hbm, rows_hbm, cols_hbm, attn_rows_hbm, attn_cols_hbm, block_ref, new_ref, attn_ref, sems,
):
    rows, cols = g_ref.shape
    attn_cols = ga_ref.shape[0]
    blocks = rows // LANES
    pairs = ((rows_ref, rows_hbm), (cols_ref, cols_hbm), (attn_rows_ref, attn_rows_hbm), (attn_cols_ref, attn_cols_hbm))
    copies = [pltpu.make_async_copy(a, b, sems.at[blocks + 1 + k]) for k, (a, b) in enumerate(pairs)]
    for copy in copies:
        copy.start()
    total = got_ref[0]
    for k in range(1, got_ref.shape[0]):
        total = total + got_ref[k]
    q_mlp, q_attn, p_mlp, p_attn = (
        jnp.sum(total[:, k * LANES : (k + 1) * LANES], axis=1, keepdims=True) for k in range(4)
    )

    def factor(q, p, count):
        clip = jnp.maximum(1.0, jnp.sqrt(jnp.broadcast_to(q, (1, LANES)) / count))
        return LEARN_RATE * jnp.sqrt(jnp.broadcast_to(p, (1, LANES)) / count) / clip

    mlp_factor, attn_factor = factor(q_mlp, p_mlp, counts[0]), factor(q_attn, p_attn, counts[1])
    along = jnp.broadcast_to(lax.rsqrt(attn_rows_ref[...].reshape(1, rows)), (SLAB, rows))
    across = lax.rsqrt(jnp.concatenate([attn_cols_ref[...].reshape(1, attn_cols), jnp.ones((1, 2 * LANES - attn_cols), F32)], axis=1))
    across = [down(across[:, k * LANES : (k + 1) * LANES] * attn_factor) for k in range(2)]
    for s in range(attn_cols // SLAB):
        at = s * SLAB
        scale = across[at // LANES][at % LANES : at % LANES + SLAB]
        new = pa_ref[pl.ds(at, SLAB), :] - ga_ref[pl.ds(at, SLAB), :].astype(F32) * wide(scale, rows) * along
        attn_ref[pl.ds(at, SLAB), :] = new
        new = new.astype(BF16)
        for k in range(block_ref.shape[0]):
            block_ref[k, pl.ds(at, SLAB), :] = new
    attn_copy = pltpu.make_async_copy(attn_ref, attn_hbm, sems.at[blocks])
    attn_copy.start()
    along = jnp.broadcast_to(lax.rsqrt(cols_ref[...].reshape(1, cols)), (SLAB, cols))
    row_scale = lax.rsqrt(rows_ref[...].reshape(1, rows))
    for b in range(blocks):
        across = down(row_scale[:, b * LANES : (b + 1) * LANES] * mlp_factor)
        for s in range(LANES // SLAB):
            at = pl.ds(b * LANES + s * SLAB, SLAB)
            scale = across[s * SLAB : (s + 1) * SLAB]
            new_ref[at, :] = p_ref[at, :] - g_ref[at, :].astype(F32) * wide(scale, cols) * along
        at = pl.ds(b * LANES, LANES)
        copies.append(pltpu.make_async_copy(new_ref.at[at], new_hbm.at[at], sems.at[b]))
        copies[-1].start()
    for copy in (attn_copy, *copies):
        copy.wait()


def assemble_kernel(got_ref, out_hbm, sems):
    rows = got_ref.shape[2]
    copies = [
        pltpu.make_async_copy(got_ref.at[k], out_hbm.at[:, pl.ds(k * rows, rows)], sems.at[k])
        for k in range(got_ref.shape[0])
    ]
    for copy in copies:
        copy.start()
    for copy in copies:
        copy.wait()


def everyone(value, axes):
    return lax.all_to_all(value, axes, 0, 0, tiled=True)


def other_core(value):
    return lax.ppermute(value, CORE, [(0, 1), (1, 0)])


def local(
    mlp_param,
    mlp_grad,
    mlp_row_state,
    mlp_col_state,
    attn_param,
    attn_grad,
    attn_row_state,
    attn_col_state,
):
    rows, cols = mlp_grad.shape
    attn_cols = attn_grad.shape[1]
    half = rows // 2
    row_devices, plane, layers = lax.axis_size(ROW), lax.axis_size(PLANE), lax.axis_size(Z)
    rows_total = rows * row_devices
    widths = (float(cols * lax.axis_size(COL)), float(attn_cols * lax.axis_size(COL)))
    counts = (rows_total * widths[0], rows_total * widths[1])
    attn_grad, attn_param = attn_grad.T, attn_param.T
    blocks = rows // LANES

    sent, row_sums, p_sums, g, ga, p, pa = call(
        sums_kernel,
        [
            pltpu.VMEM((plane, 1, 2 * rows), F32),
            pltpu.VMEM((1, 2 * rows), F32),
            pltpu.VMEM((1, 2 * LANES), F32),
            pltpu.VMEM((rows, cols), BF16),
            pltpu.VMEM((attn_cols, rows), BF16),
            pltpu.VMEM((rows, cols), F32),
            pltpu.VMEM((attn_cols, rows), F32),
        ],
        (mlp_grad, attn_grad, mlp_param, attn_param),
        in_specs=[OFF_CHIP] * 4,
        scratch=[
            pltpu.VMEM((rows + 2 * LANES, LANES), F32),
            pltpu.VMEM((8, LANES), F32),
            pltpu.SemaphoreType.DMA((2 * blocks + 2,)),
        ],
        limit=119 << 19,
    )
    got = everyone(sent, PLANE)
    cols_new, attn_cols_new, kept, sent = call(
        functools.partial(columns_kernel, float(rows_total)),
        [
            pltpu.VMEM((cols,), F32),
            pltpu.VMEM((attn_cols,), F32),
            pltpu.VMEM((1, 4 * half + 2 * LANES), F32),
            pltpu.VMEM((1, 4 * half + 2 * LANES), F32),
        ],
        (got, row_sums, p_sums, g, ga, mlp_col_state, attn_col_state),
        scratch=[pltpu.VMEM((rows, LANES), F32)],
    )
    (sent,) = call(
        spread_kernel,
        [pltpu.VMEM((layers, 1, 4 * half + 2 * LANES), F32)],
        (kept, other_core(sent)),
    )
    sent, p_sums = call(
        functools.partial(rows_kernel, widths),
        [pltpu.VMEM((1, 2 * half + 2 * LANES), F32), pltpu.VMEM((1, 2 * LANES), F32)],
        (everyone(sent, Z), mlp_row_state, attn_row_state),
    )
    rows_new, attn_rows_new, sent = call(
        scalars_kernel,
        [
            pltpu.VMEM((rows,), F32),
            pltpu.VMEM((rows,), F32),
            pltpu.VMEM((plane, 1, 4 * LANES), F32),
        ],
        (sent, other_core(sent), p_sums),
    )
    mlp_new, attn_new, rows_out, cols_out, attn_rows_out, attn_cols_out, block = call(
        functools.partial(update_kernel, counts),
        [
            jax.ShapeDtypeStruct((rows, cols), F32),
            jax.ShapeDtypeStruct((attn_cols, rows), F32),
            jax.ShapeDtypeStruct((rows,), F32),
            jax.ShapeDtypeStruct((cols,), F32),
            jax.ShapeDtypeStruct((rows,), F32),
            jax.ShapeDtypeStruct((attn_cols,), F32),
            pltpu.VMEM((row_devices, attn_cols, rows), BF16),
        ],
        (everyone(sent, PLANE), rows_new, attn_rows_new, cols_new, attn_cols_new, g, ga, p, pa),
        out_specs=[OFF_CHIP] * 6 + [ON_CHIP],
        scratch=[
            pltpu.VMEM((rows, cols), F32),
            pltpu.VMEM((attn_cols, rows), F32),
            pltpu.SemaphoreType.DMA((blocks + 5,)),
        ],
        limit=16 << 20,
    )
    (copy,) = call(
        assemble_kernel,
        [jax.ShapeDtypeStruct((attn_cols, rows_total), BF16)],
        (everyone(block, ROW),),
        out_specs=[OFF_CHIP],
        scratch=[pltpu.SemaphoreType.DMA((row_devices,))],
    )
    return (
        mlp_new,
        attn_new.T,
        rows_out,
        cols_out,
        attn_rows_out,
        attn_cols_out,
        copy.T,
    )


def solution(mesh):
    finer = Mesh(mesh.devices.reshape(4, 2, 2, 8, 2), (*ROW, *COL))
    return jax.shard_map(
        local,
        mesh=finer,
        in_specs=(
            P(ROW, COL),
            P(ROW, COL),
            P(ROW),
            P(COL),
            P(ROW, COL),
            P(ROW, COL),
            P(ROW),
            P(COL),
        ),
        out_specs=(P(ROW, COL), P(ROW, COL), P(ROW), P(COL), P(ROW), P(COL), P(None, COL)),
        check_vma=False,
    )
```

time: 135 us -> 83.2 us (0.62)
  waiting for transfers between devices: 46.7 us -> 1.65 us
  blocking collectives: 42.5 us -> 68.7 us
  starting transfers between devices: 23.4 us -> 3.93 us
  other arithmetic: 12 us -> 0 us
  Pallas kernels: 0 us -> 6.99 us
  local copies, waits for them, and re-layouts: 6.37 us -> 0.02 us
  between operations: 3.36 us -> 0.7 us
    all_to_all x0 -> x4, blocking collectives: none -> 68.7 us  [everyone(): return lax.all_to_all(value, axes, 0, 0, tiled=True)]
    all_to_all x3 -> x0, waiting for transfers between devices: 46.7 us -> none  [from_everyone(): lax.all_to_all(jnp.broadcast_to(value[None], (length, *value.shape)), axi...]
    psum x5 -> x0, blocking collectives: 42.5 us -> none  [over_axes(): value = lax.psum(value, axis)]
    all_to_all x3 -> x0, starting transfers between devices: 23.4 us -> none  [from_everyone(): lax.all_to_all(jnp.broadcast_to(value[None], (length, *value.shape)), axi...]
    reduce_sum x6 -> x0, other arithmetic: 7.48 us -> none  [the longest x2 4.2 us: local(): clip_local = (jnp.sum(jnp.square(mlp_raw)), jnp.sum(jnp.square(attn_raw)))]
    pallas_call x0 -> x7, Pallas kernels: none -> 6.99 us  [call(): pl.pallas_call(kernel, out_shape=outs, in_specs=in_specs or [ON_CHIP] * l...]
    ppermute x0 -> x2, starting transfers between devices: none -> 3.93 us  [other_core(): return lax.ppermute(value, CORE, [(0, 1), (1, 0)])]
    reshape x1 -> x0, local copies, waits for them, and re-layouts: 3.35 us -> none  [in_order(): pieces.reshape(*dims[:dim], dims[dim] * dims[dim + 1], *dims[dim + 2:])]
  transfers between devices with their start and end apart: 3 -> 2, of which waited for: 3 -> 2; matrix products, arithmetic and copies ran while one was open for 3% -> 0% of each run, Pallas kernels for 0% -> 0%
where the time goes in v2:
time: 83.2 us; the launch traced here: 82 us
  blocking collectives  68.7 us (83%)
  Pallas kernels  6.99 us (8%)
  starting transfers between devices  3.93 us (5%)
  waiting for transfers between devices  1.65 us (2%)
    all_to_all x4, blocking collectives, everyone(): return lax.all_to_all(value, axes, 0, 0, tiled=True)  68.7 us
    pallas_call x7, Pallas kernels, call(): pl.pallas_call(kernel, out_shape=outs, in_specs=in_specs or [ON_CHIP] * l...  6.99 us
    ppermute x2, starting transfers between devices, other_core(): return lax.ppermute(value, CORE, [(0, 1), (1, 0)])  3.93 us
  transfers between devices with their start and end apart: 2, of which 2 were waited for; matrix products, arithmetic and copies ran while one was open for 0% of the time, Pallas kernels for 0%

profile of v2, /device:TPU:1, one launch (start us, length us, event | category | flops | bytes accessed | tf_op | source)
XLA Modules:
  0.0 82.0 jit_solution(8965631156939213768)
XLA Ops:
  0.6 0.0 copy-start.3
  0.6 0.0 copy-start
  0.7 0.0 copy-start.1
  0.7 0.0 copy-start.2
  0.7 2.5 %shard_map.135 = (f32[16,1,1536]{2,1,0:T(1,128)S(1)}, f32[1,1536]{1,0:T(1,128)S(1)}, f32[1,256]{1,0:T(1,128)S(1)}, bf16[768,768]{1,0:T(8,128)(2,1)S(1)}, bf16[19...) custom-call(bf16[768,768]{1,0:T(8,128)(2,1)} %g_hbm.1, bf16[192,768]{1,0:T(8,128)(2,1)} %bitcast.6, ...), custom_call_target="tpu_custom_call" | custom-call | tf_op jit(solution)/shard_map/pallas_call | solution.py:30
  3.2 14.0 %all_to_all.20.got_ref = f32[16,1,1536]{2,1,0:T(1,128)S(1)} all-to-all(f32[16,1,1536]{2,1,0:T(1,128)S(1)} %get-tuple-element.30), channel_id=1, replica_groups=mesh['row_0'=4,'row_1'=2,'col_0'=2,'col_1'=8,'col_2'=2] {'col_0','row_0'..., dimensions={0} | all-to-all | bytes 196608 | tf_op jit(solution)/shard_map/all_to_all | solution.py:284
  17.3 0.0 copy-done.3
  17.3 0.0 copy-done
  17.3 0.6 shard_map.136
  17.9 2.1 %collective-permute-start = (f32[1,1792]{1,0:T(1,128)S(1)}, f32[1,1792]{1,0:T(1,128)S(1)}, u32[]{:S(2)}, u32[]{:S(2)}) collective-permute-start(f32[1,1792]{1,0:T(1,128)S(1)} %get-tuple-element.36), channel_id=1, source_target_pairs={{0,1},{1,0},{2,3},{3,2},{4,5},{5,4},{6,7},{7,6},{8,9},{9,8},{10,11... | collective-permute-start | bytes 21512 | tf_op jit(solution)/shard_map/ppermute | solution.py:288
  20.0 0.8 %collective-permute-done.got_ref = f32[1,1792]{1,0:T(1,128)S(1)} collective-permute-done((f32[1,1792]{1,0:T(1,128)S(1)}, f32[1,1792]{1,0:T(1,128)S(1)}, u32[]{:S(2)}, u32[]{:S(2)}) %collective-permute-start) | collective-permute-done | bytes 7200 | tf_op jit(solution)/shard_map/ppermute | solution.py:288
  20.8 15.1 %all_to_all.21.got_ref = f32[8,1,1792]{2,1,0:T(1,128)S(1)} all-to-all(f32[8,1,1792]{2,1,0:T(1,128)S(1)} %shard_map.137), channel_id=1, replica_groups=mesh['row_0'=4,'row_1'=2,'col_0'=2,'col_1'=8,'col_2'=2] {'col_1'}, dimensions={0} | all-to-all | bytes 114688 | tf_op jit(solution)/shard_map/all_to_all | solution.py:284
  35.9 0.0 copy-done.1
  35.9 0.0 copy-done.2
  36.0 1.9 %collective-permute-start.1 = (f32[1,1024]{1,0:T(1,128)S(1)}, f32[1,1024]{1,0:T(1,128)S(1)}, u32[]{:S(2)}, u32[]{:S(2)}) collective-permute-start(f32[1,1024]{1,0:T(1,128)S(1)} %get-tuple-element.37.own_ref), channel_id=1, source_target_pairs={{0,1},{1,0},{2,3},{3,2},{4,5},{5,4},{6,7},{7,6},{8,9},{9,8},{10,11... | collective-permute-start | bytes 12296 | tf_op jit(solution)/shard_map/ppermute | solution.py:288
  37.8 0.8 %collective-permute-done.1.got_ref = f32[1,1024]{1,0:T(1,128)S(1)} collective-permute-done((f32[1,1024]{1,0:T(1,128)S(1)}, f32[1,1024]{1,0:T(1,128)S(1)}, u32[]{:S(2)}, u32[]{:S(2)}) %collective-permute-start.1) | collective-permute-done | bytes 4128 | tf_op jit(solution)/shard_map/ppermute | solution.py:288
  38.7 9.6 %all_to_all.22.got_ref = f32[16,1,512]{2,1,0:T(1,128)S(1)} all-to-all(f32[16,1,512]{2,1,0:T(1,128)S(1)} %get-tuple-element.39), channel_id=1, replica_groups=mesh['row_0'=4,'row_1'=2,'col_0'=2,'col_1'=8,'col_2'=2] {'col_0','row_0'..., dimensions={0} | all-to-all | bytes 65536 | tf_op jit(solution)/shard_map/all_to_all | solution.py:284
  48.2 2.3 %shard_map.140 = (f32[768,768]{1,0:T(8,128)}, f32[192,768]{1,0:T(8,128)}, f32[768]{0:T(1024)}, f32[768]{0:T(1024)}, f32[768]{0:T(1024)}, /*index=5*/f32[192]{0:T(256)}, bf16[8,192,768]{2,1,0:T(8,128)(2,1)S(1)}) custom-call(f32[16,1,512]{2,1,0:T(1,128)S(1)} %all_to_all.22.got_ref, f32[768]{0:T(1024)S(1)} %get-tuple-element.40.rows_ref, ...), custom_call_target="tpu_custom_call" | custom-call | tf_op jit(solution)/shard_map/pallas_call | solution.py:30
  50.5 30.0 %all_to_all.23.got_ref = bf16[8,192,768]{2,1,0:T(8,128)(2,1)S(1)} all-to-all(bf16[8,192,768]{2,1,0:T(8,128)(2,1)S(1)} %get-tuple-element.52), channel_id=1, replica_groups=mesh['row_0'=4,'row_1'=2,'col_0'=2,'col_1'=8,'col_2'=2] {'row_0','row_1'}, dimensions={0} | all-to-all | bytes 4718592 | tf_op jit(solution)/shard_map/all_to_all | solution.py:284
  80.5 1.5 %shard_map.141 = bf16[192,6144]{1,0:T(8,128)(2,1)} custom-call(bf16[8,192,768]{2,1,0:T(8,128)(2,1)S(1)} %all_to_all.23.got_ref), custom_call_target="tpu_custom_call" | custom-call | tf_op jit(solution)/shard_map/pallas_call | solution.py:30
  (3 shorter events, 0.0 us)
Async XLA Ops:
  0.6 16.6 %copy-start.3 = (f32[192]{0:T(256)S(1)}, f32[192]{0:T(256)}, u32[]{:S(2)}) copy-start(f32[192]{0:T(256)} %attn_state_ref.2) | copy-start | bytes 2308
  0.6 16.6 %copy-start = (f32[768]{0:T(1024)S(1)}, f32[768]{0:T(1024)}, u32[]{:S(2)}) copy-start(f32[768]{0:T(1024)} %state_ref.2) | copy-start | bytes 9220
  0.7 35.3 %copy-start.1 = (f32[768]{0:T(1024)S(1)}, f32[768]{0:T(1024)}, u32[]{:S(2)}) copy-start(f32[768]{0:T(1024)} %state_ref.3) | copy-start | bytes 9220
  0.7 35.3 %copy-start.2 = (f32[768]{0:T(1024)S(1)}, f32[768]{0:T(1024)}, u32[]{:S(2)}) copy-start(f32[768]{0:T(1024)} %attn_state_ref.3) | copy-start | bytes 9220
  17.9 2.9 %collective-permute-start = (f32[1,1792]{1,0:T(1,128)S(1)}, f32[1,1792]{1,0:T(1,128)S(1)}, u32[]{:S(2)}, u32[]{:S(2)}) collective-permute-start(f32[1,1792]{1,0:T(1,128)S(1)} %get-tuple-element.36), channel_id=1, source_target_pairs={{0,1},{1,0},{2,3},{3,2},{4,5},{5,4},{6,7},{7,6},{8,9},{9,8},{10,11... | collective-permute-start | bytes 21512 | tf_op jit(solution)/shard_map/ppermute | solution.py:288
  36.0 2.7 %collective-permute-start.1 = (f32[1,1024]{1,0:T(1,128)S(1)}, f32[1,1024]{1,0:T(1,128)S(1)}, u32[]{:S(2)}, u32[]{:S(2)}) collective-permute-start(f32[1,1024]{1,0:T(1,128)S(1)} %get-tuple-element.37.own_ref), channel_id=1, source_target_pairs={{0,1},{1,0},{2,3},{3,2},{4,5},{5,4},{6,7},{7,6},{8,9},{9,8},{10,11... | collective-permute-start | bytes 12296 | tf_op jit(solution)/shard_map/ppermute | solution.py:288

commit v3 on v2

v3 whole, which is shorter than its diff:
```python
import functools

import jax
import jax.numpy as jnp
from jax import lax
from jax.experimental import pallas as pl
from jax.experimental.pallas import tpu as pltpu
from jax.sharding import Mesh
from jax.sharding import PartitionSpec as P

STEP = 4
ROW = ("row_0", "row_1")
COL = ("col_0", "col_1", "col_2")
Y_HI, Z, CORE = COL
LAYERS = (Y_HI, Z)

TINY_SQUARE = 1e-30
LEARN_RATE = 0.05
DECAY_POWER = 0.8
KEEP = 1.0 - STEP ** (-DECAY_POWER)

F32, BF16 = jnp.float32, jnp.bfloat16
SLAB = 16
LANES = 128
ON_CHIP = pl.BlockSpec(memory_space=pltpu.VMEM)
OFF_CHIP = pl.BlockSpec(memory_space=pltpu.HBM)


def call(kernel, outs, args, in_specs=None, out_specs=None, scratch=(), limit=4 << 20):
    return pl.pallas_call(
        kernel,
        out_shape=outs,
        in_specs=in_specs or [ON_CHIP] * len(args),
        out_specs=out_specs or [ON_CHIP] * len(outs),
        scratch_shapes=scratch,
        compiler_params=pltpu.CompilerParams(vmem_limit_bytes=limit),
    )(*args)


def tiles(value):
    width = value.shape[1] // LANES
    return sum((value[:, k * LANES : (k + 1) * LANES] for k in range(1, width)), value[:, :LANES])


def wide(value, width):
    return jnp.concatenate([value] * (width // LANES), axis=1)


def turned_sum(ref, start):
    return jnp.sum(ref[pl.ds(start, LANES), :].T, axis=0, keepdims=True)


def down(value):
    return jnp.broadcast_to(value, (LANES, LANES)).T


def fold(value):
    return value[:8] + value[8:]


def added(ref):
    total = ref[0]
    for k in range(1, ref.shape[0]):
        total = total + ref[k]
    return total


def sums_kernel(
    g_hbm, ga_hbm, p_hbm, pa_hbm, sent_ref, rows_ref, psum_ref, g_ref, ga_ref, p_ref, pa_ref, lane_ref, sems
):
    rows, cols = g_hbm.shape
    attn_cols = ga_hbm.shape[0]
    blocks = rows // LANES
    g_copies = [
        pltpu.make_async_copy(g_hbm.at[pl.ds(b * LANES, LANES)], g_ref.at[pl.ds(b * LANES, LANES)], sems.at[b])
        for b in range(blocks)
    ]
    p_copies = [
        pltpu.make_async_copy(
            p_hbm.at[pl.ds(b * LANES, LANES)], p_ref.at[pl.ds(b * LANES, LANES)], sems.at[blocks + b]
        )
        for b in range(blocks)
    ]
    ga_copy = pltpu.make_async_copy(ga_hbm, ga_ref, sems.at[2 * blocks])
    pa_copy = pltpu.make_async_copy(pa_hbm, pa_ref, sems.at[2 * blocks + 1])
    for copy in (*g_copies, ga_copy, *p_copies, pa_copy):
        copy.start()
    lane_ref[pl.ds(rows, 2 * LANES), :] = jnp.zeros((2 * LANES, LANES), F32)

    def squares(ref, start, first):
        def step(s, acc):
            g = ref[pl.ds(start + s * SLAB, SLAB), :].astype(F32)
            g = g * g
            lane_ref[pl.ds(first + start + s * SLAB, SLAB), :] = tiles(g)
            return acc + fold(g)

        return step

    def own_squares(ref, start):
        def step(s, acc):
            p = ref[pl.ds(start + s * SLAB, SLAB), :]
            return acc + fold(p * p)

        return step

    eight = jnp.zeros((8, cols), F32)
    steps = LANES // SLAB
    col_sum = eight
    for b, copy in enumerate(g_copies):
        copy.wait()
        col_sum = lax.fori_loop(0, steps, squares(g_ref, b * LANES, 0), col_sum, unroll=True)
        rows_ref[:, pl.ds(b * LANES, LANES)] = turned_sum(lane_ref, b * LANES)
    ga_copy.wait()
    row_sum = lax.fori_loop(0, attn_cols // SLAB, squares(ga_ref, 0, rows), jnp.zeros((8, rows), F32), unroll=4)
    rows_ref[:, pl.ds(rows, rows)] = jnp.sum(row_sum, axis=0, keepdims=True)
    rows_ref[...] += jnp.concatenate(
        [jnp.full((1, rows), cols * TINY_SQUARE, F32), jnp.full((1, rows), attn_cols * TINY_SQUARE, F32)], axis=1
    )
    col_sums = jnp.concatenate(
        [
            jnp.sum(col_sum, axis=0, keepdims=True),
            turned_sum(lane_ref, rows),
            turned_sum(lane_ref, rows + LANES),
        ],
        axis=1,
    ) + rows * TINY_SQUARE
    for k in range(sent_ref.shape[0]):
        sent_ref[k] = col_sums
    p_sum = eight
    for b, copy in enumerate(p_copies):
        copy.wait()
        p_sum = lax.fori_loop(0, steps, own_squares(p_ref, b * LANES), p_sum, unroll=True)
    pa_copy.wait()
    pa_sum = lax.fori_loop(0, attn_cols // SLAB, own_squares(pa_ref, 0), jnp.zeros((8, rows), F32), unroll=4)
    psum_ref[:, :LANES] = jnp.sum(tiles(p_sum), axis=0, keepdims=True)
    psum_ref[:, LANES:] = jnp.sum(tiles(pa_sum), axis=0, keepdims=True)


def columns_kernel(
    rows_total, got_ref, rows_ref, g_ref, ga_ref, state_ref, attn_state_ref,
    cols_ref, attn_cols_ref, kept_ref, sent_ref, lane_ref,
):
    rows, cols = g_ref.shape
    attn_cols = ga_ref.shape[0]
    half = rows // 2
    core = lax.axis_index(CORE)
    total = added(got_ref)
    row_sums = rows_ref[...]
    cols_new = KEEP * state_ref[...].reshape(1, cols) + (1.0 - KEEP) * (total[:, :cols] / rows_total)
    cols_ref[...] = cols_new.reshape(cols)
    attn_state = attn_state_ref[...].reshape(1, attn_cols)
    attn_new = KEEP * attn_state + (1.0 - KEEP) * (total[:, cols : cols + attn_cols] / rows_total)
    attn_cols_ref[...] = attn_new.reshape(attn_cols)
    inverse = jnp.broadcast_to(1.0 / cols_new, (SLAB, cols))
    attn_inverse = jnp.concatenate([1.0 / attn_new, jnp.ones((1, 2 * LANES - attn_cols), F32)], axis=1)
    down_inverse = [down(attn_inverse[:, k * LANES : (k + 1) * LANES]) for k in range(2)]

    def step(s, carry):
        g = g_ref[pl.ds(s * SLAB, SLAB), :].astype(F32)
        lane_ref[pl.ds(s * SLAB, SLAB), :] = tiles(g * g * inverse)
        return carry

    lax.fori_loop(0, rows // SLAB, step, 0, unroll=8)
    w_attn = jnp.zeros((8, rows), F32)
    for s in range(attn_cols // SLAB):
        g = ga_ref[pl.ds(s * SLAB, SLAB), :].astype(F32)
        at = s * SLAB
        scale = down_inverse[at // LANES][at % LANES : at % LANES + SLAB]
        w_attn = w_attn + fold(g * g * wide(scale, rows))
    w_attn = jnp.sum(w_attn, axis=0, keepdims=True)
    w_mlp = jnp.concatenate([turned_sum(lane_ref, b * LANES) for b in range(rows // LANES)], axis=1)
    vectors = (row_sums[:, :rows], row_sums[:, rows:], w_mlp, w_attn)
    first = jnp.concatenate([v[:, :half] for v in vectors], axis=1)
    last = jnp.concatenate([v[:, half:] for v in vectors], axis=1)
    kept_ref[...] = jnp.where(core == 0, first, last)
    sent_ref[...] = jnp.where(core == 0, last, first)


def spread_kernel(kept_ref, got_ref, psum_ref, sent_ref):
    value = jnp.concatenate([kept_ref[...] + got_ref[...], psum_ref[...]], axis=1)
    for k in range(sent_ref.shape[0]):
        sent_ref[k] = value


def rows_kernel(widths, got_ref, state_ref, attn_state_ref, sent_ref):
    rows = state_ref.shape[0]
    half = rows // 2
    core = lax.axis_index(CORE)
    total = added(got_ref)
    new, parts = [], []
    for k, (ref, width) in enumerate(zip((state_ref, attn_state_ref), widths)):
        state = ref[...].reshape(1, rows)
        state = jnp.where(core == 0, state[:, :half], state[:, half:])
        new.append(KEEP * state + (1.0 - KEEP) * (total[:, k * half : (k + 1) * half] / width))
        parts.append(tiles(total[:, (2 + k) * half : (3 + k) * half] / new[k]))
    value = jnp.concatenate([*parts, total[:, 4 * half :], *new], axis=1)
    for k in range(sent_ref.shape[0]):
        sent_ref[k] = value


def factor(got_ref, matrix, count):
    total = got_ref[0, :, : 4 * LANES]
    for k in range(1, got_ref.shape[0]):
        total = total + got_ref[k, :, : 4 * LANES]
    q, p = (
        jnp.broadcast_to(jnp.sum(total[:, k * LANES : (k + 1) * LANES], axis=1, keepdims=True), (1, LANES))
        for k in (matrix, 2 + matrix)
    )
    return LEARN_RATE * jnp.sqrt(p / count) / jnp.maximum(1.0, jnp.sqrt(q / count))


def new_rows(got_ref, matrix, half):
    row = lax.axis_index("row_0") * lax.axis_size("row_1") + lax.axis_index("row_1")
    at = pl.ds(4 * LANES + matrix * half, half)
    return jnp.concatenate([got_ref[2 * row, :, at], got_ref[2 * row + 1, :, at]], axis=1)


def attn_kernel(count, got_ref, attn_cols_ref, ga_ref, pa_ref, attn_ref, block_ref):
    attn_cols, rows = ga_ref.shape
    along = jnp.broadcast_to(lax.rsqrt(new_rows(got_ref, 1, rows // 2)), (SLAB, rows))
    across = attn_cols_ref[...].reshape(1, attn_cols)
    across = lax.rsqrt(jnp.concatenate([across, jnp.ones((1, 2 * LANES - attn_cols), F32)], axis=1))
    scale = factor(got_ref, 1, count)
    across = [down(across[:, k * LANES : (k + 1) * LANES] * scale) for k in range(2)]
    for s in range(attn_cols // SLAB):
        at = s * SLAB
        scale = across[at // LANES][at % LANES : at % LANES + SLAB]
        new = pa_ref[pl.ds(at, SLAB), :] - ga_ref[pl.ds(at, SLAB), :].astype(F32) * wide(scale, rows) * along
        attn_ref[pl.ds(at, SLAB), :] = new
        new = new.astype(BF16)
        for k in range(block_ref.shape[0]):
            block_ref[k, pl.ds(at, SLAB), :] = new


def finish_kernel(
    count, copy_ref, got_ref, cols_ref, attn_cols_ref, attn_ref, g_ref, p_ref,
    copy_hbm, attn_hbm, new_hbm, rows_hbm, cols_hbm, attn_rows_hbm, attn_cols_hbm,
    new_ref, rows_ref, attn_rows_ref, sems,
):
    rows, cols = g_ref.shape
    blocks = rows // LANES
    copies = []

    def put(source, target):
        copies.append(pltpu.make_async_copy(source, target, sems.at[len(copies)]))
        copies[-1].start()

    for k in range(copy_ref.shape[0]):
        put(copy_ref.at[k], copy_hbm.at[:, pl.ds(k * rows, rows)])
    put(attn_ref, attn_hbm)
    put(cols_ref, cols_hbm)
    put(attn_cols_ref, attn_cols_hbm)
    row_factors = new_rows(got_ref, 0, rows // 2)
    rows_ref[...] = row_factors.reshape(rows)
    attn_rows_ref[...] = new_rows(got_ref, 1, rows // 2).reshape(rows)
    along = jnp.broadcast_to(lax.rsqrt(cols_ref[...].reshape(1, cols)), (SLAB, cols))
    scale = factor(got_ref, 0, count)
    row_scale = lax.rsqrt(row_factors)
    for b in range(blocks):
        across = down(row_scale[:, b * LANES : (b + 1) * LANES] * scale)
        for s in range(LANES // SLAB):
            at = pl.ds(b * LANES + s * SLAB, SLAB)
            new_ref[at, :] = (
                p_ref[at, :] - g_ref[at, :].astype(F32) * wide(across[s * SLAB : (s + 1) * SLAB], cols) * along
            )
        at = pl.ds(b * LANES, LANES)
        put(new_ref.at[at], new_hbm.at[at])
    put(rows_ref, rows_hbm)
    put(attn_rows_ref, attn_rows_hbm)
    for copy in copies:
        copy.wait()


def everyone(value, axes):
    return lax.all_to_all(value, axes, 0, 0, tiled=True)


def other_core(value):
    return lax.ppermute(value, CORE, [(0, 1), (1, 0)])


def local(
    mlp_param,
    mlp_grad,
    mlp_row_state,
    mlp_col_state,
    attn_param,
    attn_grad,
    attn_row_state,
    attn_col_state,
):
    rows, cols = mlp_grad.shape
    attn_cols = attn_grad.shape[1]
    half = rows // 2
    row_devices, layers = lax.axis_size(ROW), lax.axis_size(LAYERS)
    message = -(-(cols + attn_cols) // LANES) * LANES
    rows_total = rows * row_devices
    widths = (float(cols * lax.axis_size(COL)), float(attn_cols * lax.axis_size(COL)))
    counts = (rows_total * widths[0], rows_total * widths[1])
    attn_grad, attn_param = attn_grad.T, attn_param.T
    blocks = rows // LANES

    sent, row_sums, p_sums, g, ga, p, pa = call(
        sums_kernel,
        [
            pltpu.VMEM((row_devices, 1, message), F32),
            pltpu.VMEM((1, 2 * rows), F32),
            pltpu.VMEM((1, 2 * LANES), F32),
            pltpu.VMEM((rows, cols), BF16),
            pltpu.VMEM((attn_cols, rows), BF16),
            pltpu.VMEM((rows, cols), F32),
            pltpu.VMEM((attn_cols, rows), F32),
        ],
        (mlp_grad, attn_grad, mlp_param, attn_param),
        in_specs=[OFF_CHIP] * 4,
        scratch=[
            pltpu.VMEM((rows + 2 * LANES, LANES), F32),
            pltpu.SemaphoreType.DMA((2 * blocks + 2,)),
        ],
        limit=119 << 19,
    )
    got = everyone(sent, ROW)
    cols_new, attn_cols_new, kept, sent = call(
        functools.partial(columns_kernel, float(rows_total)),
        [
            pltpu.VMEM((cols,), F32),
            pltpu.VMEM((attn_cols,), F32),
            pltpu.VMEM((1, 4 * half), F32),
            pltpu.VMEM((1, 4 * half), F32),
        ],
        (got, row_sums, g, ga, mlp_col_state, attn_col_state),
        scratch=[pltpu.VMEM((rows, LANES), F32)],
    )
    (sent,) = call(
        spread_kernel,
        [pltpu.VMEM((layers, 1, 4 * half + 2 * LANES), F32)],
        (kept, other_core(sent), p_sums),
    )
    (sent,) = call(
        functools.partial(rows_kernel, widths),
        [pltpu.VMEM((2 * row_devices, 1, 4 * LANES + 2 * half), F32)],
        (everyone(sent, LAYERS), mlp_row_state, attn_row_state),
    )
    got = everyone(sent, (*ROW, CORE))
    attn_new, block = call(
        functools.partial(attn_kernel, counts[1]),
        [pltpu.VMEM((attn_cols, rows), F32), pltpu.VMEM((row_devices, attn_cols, rows), BF16)],
        (got, attn_cols_new, ga, pa),
    )
    copy, attn_new, mlp_new, rows_new, cols_new, attn_rows_new, attn_cols_new = call(
        functools.partial(finish_kernel, counts[0]),
        [
            jax.ShapeDtypeStruct((attn_cols, rows_total), BF16),
            jax.ShapeDtypeStruct((attn_cols, rows), F32),
            jax.ShapeDtypeStruct((rows, cols), F32),
            jax.ShapeDtypeStruct((rows,), F32),
            jax.ShapeDtypeStruct((cols,), F32),
            jax.ShapeDtypeStruct((rows,), F32),
            jax.ShapeDtypeStruct((attn_cols,), F32),
        ],
        (everyone(block, ROW), got, cols_new, attn_cols_new, attn_new, g, p),
        out_specs=[OFF_CHIP] * 7,
        scratch=[
            pltpu.VMEM((rows, cols), F32),
            pltpu.VMEM((rows,), F32),
            pltpu.VMEM((rows,), F32),
            pltpu.SemaphoreType.DMA((row_devices + blocks + 5,)),
        ],
    )
    return mlp_new, attn_new.T, rows_new, cols_new, attn_rows_new, attn_cols_new, copy.T


def solution(mesh):
    finer = Mesh(mesh.devices.reshape(4, 2, 2, 8, 2), (*ROW, *COL))
    return jax.shard_map(
        local,
        mesh=finer,
        in_specs=(
            P(ROW, COL),
            P(ROW, COL),
            P(ROW),
            P(COL),
            P(ROW, COL),
            P(ROW, COL),
            P(ROW),
            P(COL),
        ),
        out_specs=(P(ROW, COL), P(ROW, COL), P(ROW), P(COL), P(ROW), P(COL), P(None, COL)),
        check_vma=False,
    )
```

time: 83.2 us -> 81.8 us (0.983); the launches traced: 82 us -> 81.6 us
  blocking collectives: 68.7 us -> 71.7 us
  starting transfers between devices: 3.93 us -> 2.15 us
    all_to_all x4, blocking collectives: 68.7 us -> 71.7 us  [everyone(): return lax.all_to_all(value, axes, 0, 0, tiled=True)]
    ppermute x2 -> x1, starting transfers between devices: 3.93 us -> 2.15 us  [other_core(): return lax.ppermute(value, CORE, [(0, 1), (1, 0)])]
    pallas_call x7 -> x6, Pallas kernels: 6.99 us -> 6.17 us  [call(): pl.pallas_call(kernel, out_shape=outs, in_specs=in_specs or [ON_CHIP] * l...]
  transfers between devices with their start and end apart: 2 -> 1, of which waited for: 2 -> 1; matrix products, arithmetic and copies ran while one was open for 0% -> 0% of each run, Pallas kernels for 0% -> 0%
where the time goes in v3:
time: 81.8 us; the launch traced here: 81.6 us
  blocking collectives  71.7 us (88%)
  Pallas kernels  6.17 us (8%)
  starting transfers between devices  2.15 us (3%)
  waiting for transfers between devices  0.83 us (1%)
    all_to_all x4, blocking collectives, everyone(): return lax.all_to_all(value, axes, 0, 0, tiled=True)  71.7 us
    pallas_call x6, Pallas kernels, call(): pl.pallas_call(kernel, out_shape=outs, in_specs=in_specs or [ON_CHIP] * l...  6.17 us
    ppermute x1, starting transfers between devices, other_core(): return lax.ppermute(value, CORE, [(0, 1), (1, 0)])  2.15 us
  transfers between devices with their start and end apart: 1, of which 1 were waited for; matrix products, arithmetic and copies ran while one was open for 0% of the time, Pallas kernels for 0%

profile of v3, /device:TPU:1, one launch (start us, length us, event | category | flops | bytes accessed | tf_op | source)
XLA Modules:
  0.0 81.6 jit_solution(11763339825464906790)
XLA Ops:
  0.6 0.0 copy-start.3
  0.6 0.0 copy-start
  0.7 0.0 copy-start.1
  0.7 0.0 copy-start.2
  0.7 2.5 %shard_map.135 = (f32[8,1,1024]{2,1,0:T(1,128)S(1)}, f32[1,1536]{1,0:T(1,128)S(1)}, f32[1,256]{1,0:T(1,128)S(1)}, bf16[768,768]{1,0:T(8,128)(2,1)S(1)}, bf16[192...) custom-call(bf16[768,768]{1,0:T(8,128)(2,1)} %g_hbm.1, bf16[192,768]{1,0:T(8,128)(2,1)} %bitcast.5, ...), custom_call_target="tpu_custom_call" | custom-call | tf_op jit(solution)/shard_map/pallas_call | solution.py:30
  3.2 10.8 %all_to_all.20.got_ref = f32[8,1,1024]{2,1,0:T(1,128)S(1)} all-to-all(f32[8,1,1024]{2,1,0:T(1,128)S(1)} %get-tuple-element.27), channel_id=1, replica_groups=mesh['row_0'=4,'row_1'=2,'col_0'=2,'col_1'=8,'col_2'=2] {'row_0','row_1'}, dimensions={0} | all-to-all | bytes 65536 | tf_op jit(solution)/shard_map/all_to_all | solution.py:275
  14.0 0.0 copy-done.3
  14.0 0.0 copy-done
  14.0 0.6 shard_map.136
  14.6 2.1 %collective-permute-start = (f32[1,1536]{1,0:T(1,128)S(1)}, f32[1,1536]{1,0:T(1,128)S(1)}, u32[]{:S(2)}, u32[]{:S(2)}) collective-permute-start(f32[1,1536]{1,0:T(1,128)S(1)} %get-tuple-element.32), channel_id=1, source_target_pairs={{0,1},{1,0},{2,3},{3,2},{4,5},{5,4},{6,7},{7,6},{8,9},{9,8},{10,11... | collective-permute-start | bytes 18440 | tf_op jit(solution)/shard_map/ppermute | solution.py:279
  16.8 0.8 %collective-permute-done.got_ref = f32[1,1536]{1,0:T(1,128)S(1)} collective-permute-done((f32[1,1536]{1,0:T(1,128)S(1)}, f32[1,1536]{1,0:T(1,128)S(1)}, u32[]{:S(2)}, u32[]{:S(2)}) %collective-permute-start) | collective-permute-done | bytes 6176 | tf_op jit(solution)/shard_map/ppermute | solution.py:279
  17.6 19.4 %all_to_all.21.got_ref = f32[16,1,1792]{2,1,0:T(1,128)S(1)} all-to-all(f32[16,1,1792]{2,1,0:T(1,128)S(1)} %shard_map.137), channel_id=1, replica_groups=mesh['row_0'=4,'row_1'=2,'col_0'=2,'col_1'=8,'col_2'=2] {'col_0','col_1'}, dimensions={0} | all-to-all | bytes 229376 | tf_op jit(solution)/shard_map/all_to_all | solution.py:275
  37.0 0.0 copy-done.1
  37.0 0.0 copy-done.2
  37.0 10.3 %all_to_all.22.got_ref = f32[16,1,1280]{2,1,0:T(1,128)S(1)} all-to-all(f32[16,1,1280]{2,1,0:T(1,128)S(1)} %shard_map.138), channel_id=1, replica_groups=mesh['row_0'=4,'row_1'=2,'col_0'=2,'col_1'=8,'col_2'=2] {'row_0','row_1'..., dimensions={0} | all-to-all | bytes 163840 | tf_op jit(solution)/shard_map/all_to_all | solution.py:275
  47.3 0.4 shard_map.139
  47.7 31.3 %all_to_all.23.copy_ref = bf16[8,192,768]{2,1,0:T(8,128)(2,1)S(1)} all-to-all(bf16[8,192,768]{2,1,0:T(8,128)(2,1)S(1)} %get-tuple-element.36), channel_id=1, replica_groups=mesh['row_0'=4,'row_1'=2,'col_0'=2,'col_1'=8,'col_2'=2] {'row_0','row_1'}, dimensions={0} | all-to-all | bytes 4718592 | tf_op jit(solution)/shard_map/all_to_all | solution.py:275
  79.0 2.5 %shard_map.140 = (bf16[192,6144]{1,0:T(8,128)(2,1)}, f32[192,768]{1,0:T(8,128)}, f32[768,768]{1,0:T(8,128)}, f32[768]{0:T(1024)}, f32[768]{0:T(1024)}, /*index=5*/f32[768]{0:T(1024)}, f32[192]{0:T(256)}) custom-call(bf16[8,192,768]{2,1,0:T(8,128)(2,1)S(1)} %all_to_all.23.copy_ref, f32[16,1,1280]{2,1,0:T(1,128)S(1)} %all_to_all.22.got_ref, ...), custom_call_target="tpu_custom_call" | custom-call | tf_op jit(solution)/shard_map/pallas_call | solution.py:30
  (2 shorter events, 0.1 us)
Async XLA Ops:
  0.6 13.3 %copy-start.3 = (f32[192]{0:T(256)S(1)}, f32[192]{0:T(256)}, u32[]{:S(2)}) copy-start(f32[192]{0:T(256)} %attn_state_ref.2) | copy-start | bytes 2308
  0.6 13.3 %copy-start = (f32[768]{0:T(1024)S(1)}, f32[768]{0:T(1024)}, u32[]{:S(2)}) copy-start(f32[768]{0:T(1024)} %state_ref.2) | copy-start | bytes 9220
  0.7 36.3 %copy-start.1 = (f32[768]{0:T(1024)S(1)}, f32[768]{0:T(1024)}, u32[]{:S(2)}) copy-start(f32[768]{0:T(1024)} %state_ref.3) | copy-start | bytes 9220
  0.7 36.3 %copy-start.2 = (f32[768]{0:T(1024)S(1)}, f32[768]{0:T(1024)}, u32[]{:S(2)}) copy-start(f32[768]{0:T(1024)} %attn_state_ref.3) | copy-start | bytes 9220
  14.6 3.0 %collective-permute-start = (f32[1,1536]{1,0:T(1,128)S(1)}, f32[1,1536]{1,0:T(1,128)S(1)}, u32[]{:S(2)}, u32[]{:S(2)}) collective-permute-start(f32[1,1536]{1,0:T(1,128)S(1)} %get-tuple-element.32), channel_id=1, source_target_pairs={{0,1},{1,0},{2,3},{3,2},{4,5},{5,4},{6,7},{7,6},{8,9},{9,8},{10,11... | collective-permute-start | bytes 18440 | tf_op jit(solution)/shard_map/ppermute | solution.py:279
